TPU v7x, 128 devices: a whole 4x4x4 slice. The times are simulated.
128 devices in a mesh: dp: 1, tpa: 2 (over core), tpb: 64 (over z, y, x).
Axes of the slice: x: 4, y: 4, z: 4, core: 2. Of those that a mesh axis runs over, the one named last changes fastest.
Arguments:
- hidden: bfloat16 [1024, 5, 4096], P('dp')
- w_head: bfloat16 [4096, 32768], P(None, ('tpa', 'tpb'))
- q_draft: float32 [1024, 4, 32768], P(('dp', 'tpa', 'tpb'))
- x_draft: int32 [1024, 4], P('dp')
Outputs:
- output 1: float32 [1024, 4], P('dp')
- output 2: float32 [1024], P('dp')
- output 3: float32 [1024, 4, 32768], P('dp', None, ('tpa', 'tpb'))
- output 4: float32 [1024, 32768], P('dp', ('tpa', 'tpb'))
All inputs are finite; a program needn't handle non-finite values.
Results may differ from a plain program's by a relative error of at most 0.001.
Values are sent between devices in bfloat16 or wider.
A program may use at most 1 GiB of HBM per device.

v0:
```python
import jax
import jax.numpy as jnp
from jax import lax
from jax.sharding import PartitionSpec as P

INV_TEMP = 1.25
VOCAB_AXES = ("tpa", "tpb")


def solution(mesh):
    tpb_size = mesh.shape["tpb"]

    def local_step(hidden, w_head, q_draft, x_draft):
        num_draft = x_draft.shape[1]
        vocab_local = w_head.shape[1]
        logits = jnp.einsum("bgd,dv->bgv", hidden, w_head, preferred_element_type=jnp.float32) * INV_TEMP
        glob_max = lax.pmax(jnp.max(logits, axis=-1), VOCAB_AXES)
        exp_vals = jnp.exp(logits - glob_max[..., None])
        exp_sum = lax.psum(jnp.sum(exp_vals, axis=-1), VOCAB_AXES)
        prob_all = exp_vals / exp_sum[..., None]
        q_vocab = lax.all_to_all(q_draft, VOCAB_AXES, 2, 0, tiled=True)
        p_draft = prob_all[:, :num_draft, :]
        shard_idx = lax.axis_index("tpa") * tpb_size + lax.axis_index("tpb")
        local_ids = x_draft - shard_idx * vocab_local
        is_owned = (local_ids >= 0) & (local_ids < vocab_local)
        safe_ids = jnp.clip(local_ids, 0, vocab_local - 1)[..., None]
        p_pick = jnp.where(is_owned, jnp.take_along_axis(p_draft, safe_ids, axis=2)[..., 0], 0.0)
        q_pick = jnp.where(is_owned, jnp.take_along_axis(q_vocab, safe_ids, axis=2)[..., 0], 0.0)
        excess = jnp.maximum(p_draft - q_vocab, 0.0)
        reduced = lax.psum(jnp.stack([p_pick, q_pick, jnp.sum(excess, axis=-1)]), VOCAB_AXES)
        accept = jnp.minimum(1.0, reduced[0] / reduced[1])
        expected = jnp.sum(jnp.cumprod(accept, axis=1), axis=1)
        residual = excess / reduced[2][..., None]
        return accept, expected, residual, prob_all[:, num_draft, :]

    return jax.shard_map(
        local_step, mesh=mesh,
        in_specs=(P("dp", None, None), P(None, VOCAB_AXES), P(("dp",) + VOCAB_AXES, None, None), P("dp", None)),
        out_specs=(P("dp", None), P("dp"), P("dp", None, VOCAB_AXES), P("dp", VOCAB_AXES)),
        check_vma=False)
```

profile of v0, /device:TPU:1, one launch (start us, length us, event | category | flops | bytes accessed | tf_op | source)
XLA Modules:
  0.0 742.2 jit_solution(5392957321123067125)
XLA Ops:
  0.6 43.7 %copy.95 = f32[8,4,32768]{0,1,2:T(4,128)} copy(f32[8,4,32768]{2,1,0:T(4,128)} %param.8) | data formatting | bytes 8388608 | tf_op args[2]
  44.4 81.2 %reshape.62 = f32[128,1,8192]{2,1,0:T(1,128)} reshape(f32[32768,4,8]{2,1,0:T(4,128)} %bitcast.41) | data formatting | bytes 8388608
  125.6 12.0 %all-to-all-start = ((f32[128,1,8192]{2,1,0:T(1,128)}), f32[128,1,8192]{2,1,0:T(1,128)}, u32[]{:S(2)}, u32[]{:S(2)}) async-start(f32[128,1,8192]{2,1,0:T(1,128)} %reshape.62), calls=%async_computation | async-start | bytes 8388608 | tf_op jit(solution)/shard_map/all_to_all | solution.py:21
  138.2 19.9 %multiply_reduce_fusion = (f32[1024,5]{0,1:T(8,128)S(1)}, f32[1024,5,256]{0,2,1:T(8,128)}) fusion(bf16[1024,5,4096]{2,0,1:T(8,128)(2,1)} %param.6, bf16[4096,256]{1,0:T(8,128)(2,1)S(1)} %copy-done), kind=kOutput, calls=%fused_computation.3 | convolution fusion | flops 10740034560 | bytes 49303552 | tf_op jit(solution)/shard_map/bgd,dv->bgv/dot_general | solution.py:16
  158.1 97.9 %pmax.7 = f32[1024,5]{0,1:T(8,128)S(1)} all-reduce(f32[1024,5]{0,1:T(8,128)S(1)} %get-tuple-element.40), channel_id=1, replica_groups=mesh['dp'=1,'tpa'=2,'tpb'=64] {'tpa','tpb'}, use_global_device_ids=true, to_apply=%region_1.0 | all-reduce | flops 5120 | bytes 40960 | tf_op jit(solution)/shard_map/pmax | solution.py:17
  256.0 3.4 fusion.1
  259.4 63.0 %psum.14 = f32[1024,5]{0,1:T(8,128)S(1)} all-reduce(f32[1024,5]{0,1:T(8,128)S(1)} %fusion.1), channel_id=1, replica_groups=mesh['dp'=1,'tpa'=2,'tpb'=64] {'tpa','tpb'}, use_global_device_ids=true, to_apply=%region_3.0 | all-reduce | flops 5120 | bytes 40960 | tf_op jit(solution)/shard_map/psum | solution.py:19
  322.4 3.3 fusion
  325.7 2.3 copy-done.2
  328.2 1.3 copy.102
  329.5 0.5 broadcast.76
  330.0 13.9 %reduce = f32[128,8192]{1,0:T(8,128)} reduce(f32[128,1,8192]{2,1,0:T(1,128)} %all-to-all-done, f32[]{:T(128)} %broadcast.76), dimensions={1}, to_apply=%all_to_all.13.reduce_sub_computation | reduce | bytes 8388612 | tf_op jit(solution)/shard_map/all_to_all | solution.py:21
  343.9 82.1 %reshape.63 = f32[32768,4,8]{2,1,0:T(4,128)} reshape(f32[128,8192]{1,0:T(8,128)} %reduce) | data formatting | bytes 8388608
  426.0 48.2 %copy.106 = f32[8,4,128,256]{3,0,2,1:T(8,128)} copy(f32[8,4,128,256]{0,1,3,2:T(4,128)} %bitcast.6) | data formatting | bytes 8388608 | tf_op jit(solution)/shard_map/all_to_all | solution.py:21
  474.2 5.4 copy.100
  479.6 7.4 fusion.13
  486.9 76.4 %gather_fusion.1 = f32[4096]{0:T(1024)} fusion(f32[1024,4,256]{2,0,1:T(8,128)} %bitcast.48, s32[4096]{0:T(1024)S(1)} %reshape.51), kind=kCustom, calls=%fused_computation.1.clone | custom fusion | bytes 81920 | tf_op jit(solution)/shard_map/jit(take_along_axis)/gather | solution.py:28
  563.4 70.9 %gather_fusion = f32[4096]{0:T(1024)S(1)} fusion(f32[1024,4,256]{0,2,1:T(8,128)} %get-tuple-element.36, s32[4096]{0:T(1024)S(1)} %reshape.51), kind=kCustom, calls=%fused_computation.clone | custom fusion | bytes 81920 | tf_op jit(solution)/shard_map/jit(take_along_axis)/gather | solution.py:27
  634.3 0.5 reshape.54
  635.1 0.5 reshape.60
  635.9 93.4 %psum.15 = f32[3,1024,4]{1,2,0:T(4,128)S(1)} all-reduce(f32[3,1024,4]{1,2,0:T(4,128)S(1)} %pad_maximum_fusion), channel_id=1, replica_groups=mesh['dp'=1,'tpa'=2,'tpb'=64] {'tpa','tpb'}, use_global_device_ids=true, to_apply=%region_5.7 | all-reduce | flops 12288 | bytes 98304 | tf_op jit(solution)/shard_map/psum | solution.py:30
  729.3 7.0 broadcast_divide_fusion
  736.3 5.2 copy.101
  741.5 0.6 reduce_sum.29
  (31 shorter events, 1.2 us)
Async XLA Ops:
  0.6 137.6 %copy-start = (bf16[4096,256]{1,0:T(8,128)(2,1)S(1)}, bf16[4096,256]{1,0:T(8,128)(2,1)}, u32[]{:S(2)}) copy-start(bf16[4096,256]{1,0:T(8,128)(2,1)} %param.7) | copy-start | bytes 6291460
  125.6 12.0 %copy-start.5 = (s32[1024,4]{0,1:T(4,128)S(1)}, s32[1024,4]{0,1:T(4,128)}, u32[]{:S(2)}) copy-start(s32[1024,4]{0,1:T(4,128)} %param.9) | copy-start | bytes 49156
  125.6 203.9 %all-to-all-start = ((f32[128,1,8192]{2,1,0:T(1,128)}), f32[128,1,8192]{2,1,0:T(1,128)}, u32[]{:S(2)}, u32[]{:S(2)}) async-start(f32[128,1,8192]{2,1,0:T(1,128)} %reshape.62), calls=%async_computation | async-start | bytes 8388608 | tf_op jit(solution)/shard_map/all_to_all | solution.py:21
  325.7 2.3 copy-start.2
  563.3 71.7 %copy-start.6 = (s32[1024,4]{0,1:T(4,128)S(1)}, s32[1024,4]{0,1:T(4,128)}, u32[]{:S(2)}) copy-start(s32[1024,4]{0,1:T(4,128)} %param.9) | copy-start | bytes 49156
  563.3 71.7 %copy-start.3 = (f32[4096]{0:T(1024)S(1)}, f32[4096]{0:T(1024)}, u32[]{:S(2)}) copy-start(f32[4096]{0:T(1024)} %gather_fusion.1) | copy-start | bytes 49156
  563.3 72.5 %copy-start.4 = (f32[1024,4]{0,1:T(4,128)S(1)}, f32[1024,4]{0,1:T(4,128)}, u32[]{:S(2)}) copy-start(f32[1024,4]{0,1:T(4,128)} %get-tuple-element.37) | copy-start | bytes 49156
  729.2 12.3 %copy-start.7 = (f32[1024,4]{0,1:T(4,128)}, f32[1024,4]{0,1:T(4,128)S(1)}, u32[]{:S(2)}) copy-start(f32[1024,4]{0,1:T(4,128)S(1)} %get-tuple-element.39) | copy-start | bytes 49156
  729.3 12.9 %copy-start.1 = (bf16[4096,256]{1,0:T(8,128)(2,1)S(1)}, bf16[4096,256]{1,0:T(8,128)(2,1)}, u32[]{:S(2)}) copy-start(bf16[4096,256]{1,0:T(8,128)(2,1)} %param.7) | copy-start | bytes 6291460
where the time goes:
time: 751 us; the launch traced here: 742 us
  local copies, waits for them, and re-layouts  419 us (56%)
  blocking collectives  254 us (34%)
  other arithmetic  35.7 us (5%)
  matrix products  19.9 us (3%)
  starting transfers between devices  12 us (2%)
    unnamed x21, local copies, waits for them, and re-layouts  216 us
    pmax x1, blocking collectives, local_step(): glob_max = lax.pmax(jnp.max(logits, axis=-1), VOCAB_AXES)  97.9 us
    psum x1, blocking collectives, local_step(): lax.psum(jnp.stack([p_pick, q_pick, jnp.sum(excess, axis=-1)]), VOCAB_AXES)  93.4 us
    gather x3, local copies, waits for them, and re-layouts, local_step(): jnp.take_along_axis(q_vocab, safe_ids, axis=2)[..., 0]  77.1 us
    gather x5, local copies, waits for them, and re-layouts, local_step(): jnp.take_along_axis(p_draft, safe_ids, axis=2)[..., 0]  72.1 us
    psum x1, blocking collectives, local_step(): exp_sum = lax.psum(jnp.sum(exp_vals, axis=-1), VOCAB_AXES)  63 us
    all_to_all x3, local copies, waits for them, and re-layouts, local_step(): q_vocab = lax.all_to_all(q_draft, VOCAB_AXES, 2, 0, tiled=True)  54.1 us
    dot_general x1, matrix products, local_step(): jnp.einsum('bgd,dv->bgv', hidden, w_head, preferred_element_type=jnp.floa...  19.9 us
  transfers between devices with their start and end apart: 1, of which 0 were waited for; matrix products, arithmetic and copies ran while one was open for 4% of the time, Pallas kernels for 0%

commit v1 on v0

v1 whole, which is shorter than its diff:
```python
import functools

import jax
import jax.numpy as jnp
from jax import lax
from jax.experimental import pallas as pl
from jax.experimental.pallas import tpu as pltpu
from jax.sharding import PartitionSpec as P

INV_TEMP = 1.25
VOCAB_AXES = ("tpa", "tpb")
MESH = pl.DeviceIdType.MESH
F32 = jnp.float32
LANES = 128
CHUNKS = ((0, 4), (4, 1), (5, 2), (7, 1))
ROWS = 256
NBUF = 3


def kernel(dims, h_ref, w_ref, q_ref, x_ref, acc_ref, exp_ref, res_ref, bon_ref,
           hbuf, wbuf, qsrc, qdst, zr, z4, zb, st_send, st_recv, ag_send, ag_recv, zs_send, zs_recv, za_send, za_recv,
           zb_recv, h_sem, w_sem, q_sem, out_sem, bulk_ss, bulk_rs, st_ss, st_rs, ag_ss, ag_rs, zs_ss, zs_rs, za_ss,
           za_rs, zc_ss, zc_rs):
    na, nb = dims
    nd = na * nb
    me_a, me_b = lax.axis_index("tpa"), lax.axis_index("tpb")
    me = me_a * nb + me_b
    npos = h_ref.shape[0]
    ndraft = npos - 1
    nseq = h_ref.shape[1]
    nblk = nseq // LANES
    nunit = nblk * npos
    per_src = nseq // nd
    vloc = w_ref.shape[1]

    def dev(f):
        return {"tpa": f // nb, "tpb": f % nb}

    def peer(k):
        ka, kb = k % na, k // na
        kx, ky, kz = kb % 4, (kb // 4) % 4, kb // 16
        x, y, z = me_b % 4, (me_b // 4) % 4, me_b // 16
        b = ((z + kz) % 4) * 16 + ((y + ky) % 4) * 4 + (x + kx) % 4
        return ((me_a + ka) % na) * nb + b

    def each_peer(fn):
        def body(k, carry):
            fn(peer(k))
            return carry
        lax.fori_loop(1, nd, body, 0)

    lane = lax.broadcasted_iota(jnp.int32, (8, LANES), 1)
    sub = lax.broadcasted_iota(jnp.int32, (8, LANES), 0)
    sub4 = lax.broadcasted_iota(jnp.int32, (4, LANES), 0)
    lane_f = lane.astype(F32)
    eye = (lax.broadcasted_iota(jnp.int32, (LANES, LANES), 0) == lax.broadcasted_iota(jnp.int32, (LANES, LANES), 1))

    def to_col(row):
        return jnp.sum(jnp.where(eye, jnp.broadcast_to(row, (LANES, LANES)), 0.0), axis=1, keepdims=True)

    def to_row(col):
        return jnp.sum(jnp.where(eye, jnp.broadcast_to(col, (LANES, LANES)), 0.0), axis=0, keepdims=True)

    def twice(t):
        return jnp.concatenate([t, t], axis=0)

    q_copy = pltpu.make_async_copy(q_ref, qsrc, q_sem)
    q_copy.start()
    w_copy = pltpu.make_async_copy(w_ref, wbuf, w_sem)
    w_copy.start()
    per_pos = nseq // ROWS

    def h_copy(t):
        return pltpu.make_async_copy(h_ref.at[t // per_pos, pl.ds((t % per_pos) * ROWS, ROWS)], hbuf.at[t % NBUF],
                                     h_sem.at[t % NBUF])

    for t in range(NBUF - 1):
        h_copy(t).start()

    barrier = pltpu.get_barrier_semaphore()
    each_peer(lambda f: pl.semaphore_signal(barrier, inc=1, device_id=dev(f), device_id_type=MESH))
    q_copy.wait()

    def local_bulk(g):
        c0, n = CHUNKS[g]
        return pltpu.make_async_copy(qsrc.at[pl.ds(c0, n), me], qdst.at[me, pl.ds(c0, n)], bulk_rs.at[g])

    for g in range(len(CHUNKS)):
        local_bulk(g).start()
    pl.semaphore_wait(barrier, nd - 1)

    def send_bulk(g):
        c0, n = CHUNKS[g]
        each_peer(lambda f: pltpu.make_async_remote_copy(
            src_ref=qsrc.at[pl.ds(c0, n), f], dst_ref=qdst.at[me, pl.ds(c0, n)], send_sem=bulk_ss.at[g],
            recv_sem=bulk_rs.at[g], device_id=dev(f), device_id_type=MESH).start())

    def wait_bulk(g):
        c0, n = CHUNKS[g]
        ref = qdst.at[:, pl.ds(c0, n)]
        pltpu.make_async_copy(ref, ref, bulk_rs.at[g]).wait()

    send_bulk(0)

    xb = x_ref[:, pl.ds(pl.multiple_of((me // 16) * LANES, LANES), LANES)].astype(F32)
    targets = []
    for c in range(per_src):
        j = (me % 16) * per_src + c
        col = jnp.sum(jnp.where(lane[:4] == j, xb, 0.0), axis=1, keepdims=True)
        targets.append(twice(jnp.broadcast_to(col, (4, LANES))) - jnp.where(sub >= 4, F32(LANES), F32(0)) - lane_f)

    def pick_q(d, accs):
        base = (d * vloc).astype(F32)
        return tuple(a + jnp.where(t == base, qsrc[c, d], 0.0) for c, (a, t) in enumerate(zip(accs, targets)))

    accs = lax.fori_loop(0, nd, pick_q, tuple(jnp.zeros((8, LANES), F32) for _ in range(per_src)))
    qp = jnp.zeros((4, LANES), F32)
    for c in range(per_src):
        col = jnp.sum(accs[c], axis=1, keepdims=True)
        qp = jnp.where(lane[:4] == (me % 16) * per_src + c, col[:4] + col[4:], qp)

    w_copy.wait()
    my_base = (me * vloc).astype(F32)
    lane2 = lax.broadcasted_iota(jnp.int32, (LANES, vloc), 1).astype(F32)

    def matmul(t, carry):
        @pl.when(t + NBUF - 1 < npos * per_pos)
        def _():
            h_copy(t + NBUF - 1).start()

        h_copy(t).wait()
        i, r = t // per_pos, t % per_pos
        zb[...] = jnp.dot(hbuf[t % NBUF], wbuf[...], preferred_element_type=F32) * INV_TEMP
        for half in range(ROWS // LANES):
            blk = r * (ROWS // LANES) + half
            zz = zb[half * LANES:(half + 1) * LANES, :]
            m = jnp.max(zz, axis=1, keepdims=True)
            s = jnp.sum(jnp.exp(zz - m), axis=1, keepdims=True)
            ii = jnp.minimum(i, ndraft - 1)
            xblk = x_ref[:, pl.ds(pl.multiple_of(blk * LANES, LANES), LANES)].astype(F32)
            xrow = jnp.sum(jnp.where(sub4 == ii, xblk, 0.0), axis=0, keepdims=True) - my_base
            pick = jnp.sum(jnp.where(lane2 == to_col(xrow), zz, 0.0), axis=1, keepdims=True)
            qrow = jnp.sum(jnp.where((sub4 == ii) & (blk == me // 16), qp, 0.0), axis=0, keepdims=True)
            tile = jnp.where(sub4 == 0, to_row(m), jnp.where(sub4 == 1, to_row(s), jnp.where(
                sub4 == 2, to_row(pick), qrow)))
            st_send[blk * npos + i] = tile

            @pl.when(i < ndraft)
            def _():
                for lt in range(vloc // LANES):
                    zr[pl.ds(blk * LANES * 8 + lt * 4 + i, LANES, stride=8), :] = zz[:, lt * LANES:(lt + 1) * LANES]

            @pl.when(i == ndraft)
            def _():
                z4[pl.ds(pl.multiple_of(blk * LANES, LANES), LANES), :] = zz
        return carry

    lax.fori_loop(0, npos * per_pos, matmul, 0)

    def owner(u):
        return u * 3

    is_owner = (me % 3 == 0) & (me < nunit * 3)
    my_unit = me // 3

    def send_stats(u, carry):
        f = owner(u)

        @pl.when(f != me)
        def _():
            pltpu.make_async_remote_copy(src_ref=st_send.at[u], dst_ref=st_recv.at[me], send_sem=st_ss, recv_sem=st_rs,
                                         device_id=dev(f), device_id_type=MESH).start()
        return carry

    lax.fori_loop(0, nunit, send_stats, 0)
    send_bulk(1)

    @pl.when(is_owner)
    def _():
        pltpu.make_async_copy(st_send.at[my_unit], st_recv.at[me], st_rs).start()
        pltpu.make_async_copy(st_recv, st_recv, st_rs).wait()
        mx = lax.fori_loop(0, nd, lambda s, m: jnp.maximum(m, st_recv[s]), st_recv[0])[0:1]

        def add(s, carry):
            t = st_recv[s]
            es, zp, qq = carry
            return es + jnp.exp(t[0:1] - mx) * t[1:2], zp + t[2:3], qq + t[3:4]

        zero = jnp.zeros((1, LANES), F32)
        es, zp, qq = lax.fori_loop(0, nd, add, (zero, zero, zero))
        accept = jnp.minimum(1.0, jnp.exp(zp - mx) / es / qq)
        ag_send[...] = jnp.where(sub4 == 0, mx, jnp.where(sub4 == 1, 1.0 / es, accept))
        pltpu.make_async_copy(ag_send, ag_recv.at[my_unit], ag_rs).start()
        each_peer(lambda f: pltpu.make_async_remote_copy(
            src_ref=ag_send, dst_ref=ag_recv.at[my_unit], send_sem=ag_ss, recv_sem=ag_rs, device_id=dev(f),
            device_id_type=MESH).start())

    send_bulk(2)

    pltpu.make_async_copy(ag_recv, ag_recv, ag_rs).wait()

    def probs(blk, carry):
        def rows(k):
            return jnp.concatenate([ag_recv[blk * npos + i, k:k + 1, :] for i in range(ndraft)], axis=0)

        m8, r8, a4 = twice(rows(0)), twice(rows(1)), rows(2)
        cols = pl.ds(pl.multiple_of(blk * LANES, LANES), LANES)
        acc_ref[:, cols] = a4
        run, tot = a4[0:1], a4[0:1]
        for i in range(1, ndraft):
            run = run * a4[i:i + 1]
            tot = tot + run
        exp_ref[:, cols] = tot
        for j in range(LANES):
            at = pl.ds(pl.multiple_of((blk * LANES + j) * 8, 8), 8)
            zr[at, :] = jnp.exp(zr[at, :] - m8[:, j:j + 1]) * r8[:, j:j + 1]
        u4 = blk * npos + ndraft
        z4[cols, :] = jnp.exp(z4[cols, :] - to_col(ag_recv[u4, 0:1, :])) * to_col(ag_recv[u4, 1:2, :])
        return carry

    lax.fori_loop(0, nblk, probs, 0)
    bon_copy = pltpu.make_async_copy(z4, bon_ref, out_sem)
    bon_copy.start()

    def excess(g):
        c0, n = CHUNKS[g]

        def body(s, accs):
            new = []
            for c in range(n):
                at = pl.ds(pl.multiple_of((s * per_src + c0 + c) * 8, 8), 8)
                e = jnp.maximum(zr[at, :] - qdst[s, c0 + c], 0.0)
                zr[at, :] = e
                new.append(jnp.where(lane == s, jnp.sum(e, axis=1, keepdims=True), accs[c]))
            return tuple(new)

        accs = lax.fori_loop(0, nd, body, tuple(jnp.zeros((8, LANES), F32) for _ in range(n)), unroll=4)
        for c in range(n):
            zs_send[c0 + c] = accs[c][:4] + accs[c][4:]

    def z_owner(c):
        return (c * 16 + 5) % nd

    def send_sums(g):
        c0, n = CHUNKS[g]
        for c in range(c0, c0 + n):
            @pl.when(me != z_owner(c))
            def _():
                pltpu.make_async_remote_copy(src_ref=zs_send.at[c], dst_ref=zs_recv.at[me], send_sem=zs_ss,
                                             recv_sem=zs_rs, device_id=dev(z_owner(c)), device_id_type=MESH).start()

    def sum_of(ref):
        return lax.fori_loop(0, nd, lambda s, a: a + ref[s], jnp.zeros((4, LANES), F32), unroll=8)

    def own_sums(g):
        c0, n = CHUNKS[g]
        for c in range(c0, c0 + n):
            @pl.when(me == z_owner(c))
            def _():
                pltpu.make_async_copy(zs_send.at[c], zs_recv.at[me], zs_rs).start()
                pltpu.make_async_copy(zs_recv, zs_recv, zs_rs).wait()
                za_send[...] = sum_of(zs_recv)
                pltpu.make_async_copy(za_send, za_recv.at[c], za_rs.at[g]).start()
                each_peer(lambda f: pltpu.make_async_remote_copy(
                    src_ref=za_send, dst_ref=za_recv.at[c], send_sem=za_ss, recv_sem=za_rs.at[g], device_id=dev(f),
                    device_id_type=MESH).start())

    def wait_sums(g):
        c0, n = CHUNKS[g]
        ref = za_recv.at[pl.ds(c0, n)]
        pltpu.make_async_copy(ref, ref, za_rs.at[g]).wait()

    def scale(c, tile):
        r8 = twice(1.0 / tile)
        for s in range(nd):
            at = pl.ds((s * per_src + c) * 8, 8)
            zr[at, :] = zr[at, :] * r8[:, s:s + 1]

    zr4 = zr.reshape(nd, per_src, 8, LANES)

    def put(g):
        c0, n = CHUNKS[g]
        return pltpu.make_async_copy(zr4.at[:, pl.ds(c0, n)], res_ref.at[:, pl.ds(c0, n)], out_sem)

    def finish(g):
        c0, n = CHUNKS[g]

        def one(c, carry):
            scale(c, za_recv[c])
            return carry

        lax.fori_loop(c0, c0 + n, one, 0)
        put(g).start()

    last = len(CHUNKS) - 1
    for g in range(2):
        wait_bulk(g)
        excess(g)
        send_sums(g)
    send_bulk(3)
    for g in range(2):
        own_sums(g)
    wait_bulk(2)
    excess(2)
    send_sums(2)
    own_sums(2)
    for g in range(2):
        wait_sums(g)
        finish(g)
    wait_bulk(last)
    excess(last)
    c_last = CHUNKS[last][0]
    pltpu.make_async_copy(zs_send.at[c_last], zb_recv.at[me], zc_rs).start()
    each_peer(lambda f: pltpu.make_async_remote_copy(
        src_ref=zs_send.at[c_last], dst_ref=zb_recv.at[me], send_sem=zc_ss, recv_sem=zc_rs, device_id=dev(f),
        device_id_type=MESH).start())
    wait_sums(2)
    finish(2)
    pltpu.make_async_copy(zb_recv, zb_recv, zc_rs).wait()
    scale(c_last, sum_of(zb_recv))
    put(last).start()

    def drain(ref, sem):
        pltpu.make_async_copy(ref, ref, sem).wait()

    for g, (c0, n) in enumerate(CHUNKS):
        drain(qsrc.at[pl.ds(c0, n), pl.ds(0, nd - 1)], bulk_ss.at[g])

    @pl.when(is_owner)
    def _():
        drain(st_send.at[pl.ds(0, nunit - 1)], st_ss)
        drain(st_recv.at[pl.ds(0, nd - 1)], ag_ss)

    @pl.when(jnp.logical_not(is_owner))
    def _():
        drain(st_send, st_ss)

    nz = c_last
    is_zowner = (me % 16 == 5) & (me // 16 < nz)

    @pl.when(is_zowner)
    def _():
        drain(zs_send.at[pl.ds(0, nz - 1)], zs_ss)
        drain(st_recv.at[pl.ds(0, nd - 1)], za_ss)

    @pl.when(jnp.logical_not(is_zowner))
    def _():
        drain(zs_send.at[pl.ds(0, nz)], zs_ss)

    drain(st_recv.at[pl.ds(0, nd - 1)], zc_ss)
    bon_copy.wait()
    for g in range(len(CHUNKS)):
        put(g).wait()


def solution(mesh):
    na, nb = mesh.shape["tpa"], mesh.shape["tpb"]
    nd = na * nb

    def local_step(hidden, w_head, q_draft, x_draft):
        nseq, npos, dm = hidden.shape
        ndraft = npos - 1
        vloc = w_head.shape[1]
        per_src = q_draft.shape[0]
        nt = vloc // LANES
        h5 = jnp.transpose(hidden, (1, 0, 2))
        q4 = q_draft.reshape(per_src, ndraft, nd, nt, LANES).transpose(0, 2, 3, 1, 4).reshape(per_src, nd, nt * ndraft,
                                                                                             LANES)
        xt = x_draft.T
        nunit = (nseq // LANES) * npos
        any_ = pl.BlockSpec(memory_space=pl.ANY)
        vmem = pl.BlockSpec(memory_space=pltpu.VMEM)
        dma, vm = pltpu.SemaphoreType.DMA, pltpu.VMEM
        acc, exp, res, bonus = pl.pallas_call(
            functools.partial(kernel, (na, nb)),
            out_shape=[
                jax.ShapeDtypeStruct((ndraft, nseq), F32),
                jax.ShapeDtypeStruct((1, nseq), F32),
                jax.ShapeDtypeStruct((nd, per_src, nt * ndraft, LANES), F32),
                jax.ShapeDtypeStruct((nseq, vloc), F32),
            ],
            in_specs=[any_, any_, any_, vmem],
            out_specs=[vmem, vmem, any_, any_],
            scratch_shapes=[
                vm((NBUF, ROWS, dm), jnp.bfloat16),
                vm((dm, vloc), jnp.bfloat16),
                vm((per_src, nd, 8, LANES), F32),
                vm((nd, per_src, 8, LANES), F32),
                vm((nseq * 8, LANES), F32),
                vm((nseq, vloc), F32),
                vm((ROWS, vloc), F32),
                vm((nunit, 4, LANES), F32),
                vm((nd, 4, LANES), F32),
                vm((4, LANES), F32),
                vm((nunit, 4, LANES), F32),
                vm((per_src, 4, LANES), F32),
                vm((nd, 4, LANES), F32),
                vm((4, LANES), F32),
                vm((per_src, 4, LANES), F32),
                vm((nd, 4, LANES), F32),
                dma((NBUF,)), dma, dma, dma, dma((len(CHUNKS),)), dma((len(CHUNKS),)), dma, dma, dma, dma, dma, dma,
                dma, dma((len(CHUNKS) - 1,)), dma, dma,
            ],
            compiler_params=pltpu.CompilerParams(collective_id=0, has_side_effects=True,
                                                 vmem_limit_bytes=48 * 1024 * 1024),
            name="verify",
        )(h5, w_head, q4, xt)
        residual = res.reshape(nseq, nt, ndraft, LANES).transpose(0, 2, 1, 3).reshape(nseq, ndraft, vloc)
        return acc.T, exp.reshape(nseq), residual, bonus

    return jax.shard_map(
        local_step, mesh=mesh,
        in_specs=(P("dp", None, None), P(None, VOCAB_AXES), P(("dp",) + VOCAB_AXES, None, None), P("dp", None)),
        out_specs=(P("dp", None), P("dp"), P("dp", None, VOCAB_AXES), P("dp", VOCAB_AXES)),
        check_vma=False)
```

time: 751 us -> 136 us (0.18); the launches traced: 742 us -> 136 us
  local copies, waits for them, and re-layouts: 419 us -> 9.39 us
  blocking collectives: 254 us -> 0 us
  Pallas kernels: 0 us -> 126 us
  other arithmetic: 35.7 us -> 0 us
  matrix products: 19.9 us -> 0 us
  starting transfers between devices: 12 us -> 0 us
    unnamed x21 -> x8, local copies, waits for them, and re-layouts: 216 us -> 9.39 us
    psum x2 -> x0, blocking collectives: 156 us -> none  [the longest x1 93.4 us: local_step(): lax.psum(jnp.stack([p_pick, q_pick, jnp.sum(excess, axis=-1)]), VOCAB_AXES)]
    gather x8 -> x0, local copies, waits for them, and re-layouts: 149 us -> none  [the longest x3 77.1 us: local_step(): jnp.take_along_axis(q_vocab, safe_ids, axis=2)[..., 0]]
    pallas_call x0 -> x1, Pallas kernels: none -> 126 us  [local_step(): pl.pallas_call(functools.partial(kernel, (na, nb)), out_shape=[jax.ShapeD...]
    pmax x1 -> x0, blocking collectives: 97.9 us -> none  [local_step(): glob_max = lax.pmax(jnp.max(logits, axis=-1), VOCAB_AXES)]
    all_to_all x3 -> x0, local copies, waits for them, and re-layouts: 54.1 us -> none  [local_step(): q_vocab = lax.all_to_all(q_draft, VOCAB_AXES, 2, 0, tiled=True)]
    dot_general x1 -> x0, matrix products: 19.9 us -> none  [local_step(): jnp.einsum('bgd,dv->bgv', hidden, w_head, preferred_element_type=jnp.floa...]
    all_to_all x1 -> x0, other arithmetic: 13.9 us -> none  [local_step(): q_vocab = lax.all_to_all(q_draft, VOCAB_AXES, 2, 0, tiled=True)]
  transfers between devices with their start and end apart: 1 -> 0, of which waited for: 0 -> 0; matrix products, arithmetic and copies ran while one was open for 4% -> 0% of each run, Pallas kernels for 0% -> 0%
where the time goes in v1:
time: 136 us
  Pallas kernels  126 us (93%)
  local copies, waits for them, and re-layouts  9.39 us (7%)
    pallas_call x1, Pallas kernels, local_step(): pl.pallas_call(functools.partial(kernel, (na, nb)), out_shape=[jax.ShapeD...  126 us
    unnamed x8, local copies, waits for them, and re-layouts  9.39 us

profile of v1, /device:TPU:1, one launch (start us, length us, event | category | flops | bytes accessed | tf_op | source)
XLA Modules:
  0.0 135.9 jit_solution(9202150814356512822)
XLA Ops:
  0.6 0.0 copy-start
  0.6 1.6 %copy-done = bf16[4096,256]{1,0:T(8,128)(2,1)S(1)} copy-done((bf16[4096,256]{1,0:T(8,128)(2,1)S(1)}, bf16[4096,256]{1,0:T(8,128)(2,1)}, u32[]{:S(2)}) %copy-start) | copy-done | bytes 2097176
  2.2 0.0 copy-start.1
  2.2 0.7 copy-done.1
  2.9 125.9 %verify.1 = (f32[4,1024]{1,0:T(4,128)S(1)}, f32[1,1024]{1,0:T(1,128)S(1)}, f32[128,8,8,128]{3,2,1,0:T(8,128)}, f32[1024,256]{1,0:T(8,128)S(1)}) custom-call(bf16[5,1024,4096]{2,1,0:T(8,128)(2,1)} %bitcast.17, bf16[4096,256]{1,0:T(8,128)(2,1)S(1)} %copy-done, f32[8,128,8,128]{3,2,1,0:T(8,128)} %bitcast.19, s32[4,1024]{1,0:T(4,128)S(1)} %bitcast.14), custom_call_target="tpu_custom_call" | custom-call | tf_op jit(solution)/shard_map/verify/pallas_call | solution.py:374
  128.8 0.6 copy.14
  129.4 0.6 copy.15
  130.0 4.9 %copy.16 = f32[1024,4,256]{2,1,0:T(4,128)} copy(f32[1024,4,256]{2,1,0:T(4,128)} %bitcast.18) | data formatting | bytes 8388608
  134.9 1.0 copy.17
Async XLA Ops:
  0.6 1.6 %copy-start = (bf16[4096,256]{1,0:T(8,128)(2,1)S(1)}, bf16[4096,256]{1,0:T(8,128)(2,1)}, u32[]{:S(2)}) copy-start(bf16[4096,256]{1,0:T(8,128)(2,1)} %w_ref.1) | copy-start | bytes 6291460
  2.2 0.7 copy-start.1

commit v2 on v1

--- a/solution.py
+++ b/solution.py
@@ -17,9 +17,9 @@
 NBUF = 3
 
 
-def kernel(dims, h_ref, w_ref, q_ref, x_ref, acc_ref, exp_ref, res_ref, bon_ref,
-           hbuf, wbuf, qsrc, qdst, zr, z4, zb, st_send, st_recv, ag_send, ag_recv, zs_send, zs_recv, za_send, za_recv,
-           zb_recv, h_sem, w_sem, q_sem, out_sem, bulk_ss, bulk_rs, st_ss, st_rs, ag_ss, ag_rs, zs_ss, zs_rs, za_ss,
+def kernel(dims, h_ref, w_ref, q_ref, xin_ref, acc_ref, exp_ref, zr, z4,
+           hbuf, wbuf, x_ref, qsrc, qdst, zb, st_send, st_recv, ag_send, ag_recv, zs_send, zs_recv, za_send, za_recv,
+           zb_recv, h_sem, w_sem, q_sem, x_sem, bulk_ss, bulk_rs, st_ss, st_rs, ag_ss, ag_rs, zs_ss, zs_rs, za_ss,
            za_rs, zc_ss, zc_rs):
     na, nb = dims
     nd = na * nb
@@ -36,18 +36,29 @@
     def dev(f):
         return {"tpa": f // nb, "tpb": f % nb}
 
-    def peer(k):
-        ka, kb = k % na, k // na
-        kx, ky, kz = kb % 4, (kb // 4) % 4, kb // 16
-        x, y, z = me_b % 4, (me_b // 4) % 4, me_b // 16
-        b = ((z + kz) % 4) * 16 + ((y + ky) % 4) * 4 + (x + kx) % 4
-        return ((me_a + ka) % na) * nb + b
+    px, py, pz = me_b % 4, (me_b // 4) % 4, me_b // 16
+    xs = [(px + k) % 4 for k in range(4)]
+    ys = [((py + k) % 4) * 4 for k in range(4)]
+    cores = [me_a, (me_a + 1) % na]
 
     def each_peer(fn):
-        def body(k, carry):
-            fn(peer(k))
+        def plane(kz, carry):
+            zz = pz + kz
+            base = jnp.where(zz >= 4, zz - 4, zz) * 16
+            for ky in range(4):
+                for kx in (1, 3, 2, 0):
+                    for ka in range(na):
+                        b = base + ys[ky] + xs[kx]
+                        f = cores[ka] * nb + b
+                        ident = {"tpa": cores[ka], "tpb": b}
+                        if ka == kx == ky == 0:
+                            @pl.when(kz > 0)
+                            def _():
+                                fn(f, ident)
+                        else:
+                            fn(f, ident)
             return carry
-        lax.fori_loop(1, nd, body, 0)
+        lax.fori_loop(0, 4, plane, 0)
 
     lane = lax.broadcasted_iota(jnp.int32, (8, LANES), 1)
     sub = lax.broadcasted_iota(jnp.int32, (8, LANES), 0)
@@ -74,11 +85,13 @@
         return pltpu.make_async_copy(h_ref.at[t // per_pos, pl.ds((t % per_pos) * ROWS, ROWS)], hbuf.at[t % NBUF],
                                      h_sem.at[t % NBUF])
 
+    x_copy = pltpu.make_async_copy(xin_ref, x_ref, x_sem)
+    x_copy.start()
     for t in range(NBUF - 1):
         h_copy(t).start()
 
     barrier = pltpu.get_barrier_semaphore()
-    each_peer(lambda f: pl.semaphore_signal(barrier, inc=1, device_id=dev(f), device_id_type=MESH))
+    each_peer(lambda f, ident: pl.semaphore_signal(barrier, inc=1, device_id=ident, device_id_type=MESH))
     q_copy.wait()
 
     def local_bulk(g):
@@ -91,9 +104,14 @@
 
     def send_bulk(g):
         c0, n = CHUNKS[g]
-        each_peer(lambda f: pltpu.make_async_remote_copy(
-            src_ref=qsrc.at[pl.ds(c0, n), f], dst_ref=qdst.at[me, pl.ds(c0, n)], send_sem=bulk_ss.at[g],
-            recv_sem=bulk_rs.at[g], device_id=dev(f), device_id_type=MESH).start())
+
+        def one(c, carry):
+            each_peer(lambda f, ident: pltpu.make_async_remote_copy(
+                src_ref=qsrc.at[c, f], dst_ref=qdst.at[me, c], send_sem=bulk_ss.at[g], recv_sem=bulk_rs.at[g],
+                device_id=ident, device_id_type=MESH).start())
+            return carry
+
+        lax.fori_loop(c0, c0 + n, one, 0)
 
     def wait_bulk(g):
         c0, n = CHUNKS[g]
@@ -102,6 +120,7 @@
 
     send_bulk(0)
 
+    x_copy.wait()
     xb = x_ref[:, pl.ds(pl.multiple_of((me // 16) * LANES, LANES), LANES)].astype(F32)
     targets = []
     for c in range(per_src):
@@ -191,8 +210,8 @@
         accept = jnp.minimum(1.0, jnp.exp(zp - mx) / es / qq)
         ag_send[...] = jnp.where(sub4 == 0, mx, jnp.where(sub4 == 1, 1.0 / es, accept))
         pltpu.make_async_copy(ag_send, ag_recv.at[my_unit], ag_rs).start()
-        each_peer(lambda f: pltpu.make_async_remote_copy(
-            src_ref=ag_send, dst_ref=ag_recv.at[my_unit], send_sem=ag_ss, recv_sem=ag_rs, device_id=dev(f),
+        each_peer(lambda f, ident: pltpu.make_async_remote_copy(
+            src_ref=ag_send, dst_ref=ag_recv.at[my_unit], send_sem=ag_ss, recv_sem=ag_rs, device_id=ident,
             device_id_type=MESH).start())
 
     send_bulk(2)
@@ -219,8 +238,6 @@
         return carry
 
     lax.fori_loop(0, nblk, probs, 0)
-    bon_copy = pltpu.make_async_copy(z4, bon_ref, out_sem)
-    bon_copy.start()
 
     def excess(g):
         c0, n = CHUNKS[g]
@@ -261,8 +278,8 @@
                 pltpu.make_async_copy(zs_recv, zs_recv, zs_rs).wait()
                 za_send[...] = sum_of(zs_recv)
                 pltpu.make_async_copy(za_send, za_recv.at[c], za_rs.at[g]).start()
-                each_peer(lambda f: pltpu.make_async_remote_copy(
-                    src_ref=za_send, dst_ref=za_recv.at[c], send_sem=za_ss, recv_sem=za_rs.at[g], device_id=dev(f),
+                each_peer(lambda f, ident: pltpu.make_async_remote_copy(
+                    src_ref=za_send, dst_ref=za_recv.at[c], send_sem=za_ss, recv_sem=za_rs.at[g], device_id=ident,
                     device_id_type=MESH).start())
 
     def wait_sums(g):
@@ -276,12 +293,6 @@
             at = pl.ds((s * per_src + c) * 8, 8)
             zr[at, :] = zr[at, :] * r8[:, s:s + 1]
 
-    zr4 = zr.reshape(nd, per_src, 8, LANES)
-
-    def put(g):
-        c0, n = CHUNKS[g]
-        return pltpu.make_async_copy(zr4.at[:, pl.ds(c0, n)], res_ref.at[:, pl.ds(c0, n)], out_sem)
-
     def finish(g):
         c0, n = CHUNKS[g]
 
@@ -290,7 +301,6 @@
             return carry
 
         lax.fori_loop(c0, c0 + n, one, 0)
-        put(g).start()
 
     last = len(CHUNKS) - 1
     for g in range(2):
@@ -311,14 +321,13 @@
     excess(last)
     c_last = CHUNKS[last][0]
     pltpu.make_async_copy(zs_send.at[c_last], zb_recv.at[me], zc_rs).start()
-    each_peer(lambda f: pltpu.make_async_remote_copy(
-        src_ref=zs_send.at[c_last], dst_ref=zb_recv.at[me], send_sem=zc_ss, recv_sem=zc_rs, device_id=dev(f),
+    each_peer(lambda f, ident: pltpu.make_async_remote_copy(
+        src_ref=zs_send.at[c_last], dst_ref=zb_recv.at[me], send_sem=zc_ss, recv_sem=zc_rs, device_id=ident,
         device_id_type=MESH).start())
     wait_sums(2)
     finish(2)
     pltpu.make_async_copy(zb_recv, zb_recv, zc_rs).wait()
     scale(c_last, sum_of(zb_recv))
-    put(last).start()
 
     def drain(ref, sem):
         pltpu.make_async_copy(ref, ref, sem).wait()
@@ -348,9 +357,14 @@
         drain(zs_send.at[pl.ds(0, nz)], zs_ss)
 
     drain(st_recv.at[pl.ds(0, nd - 1)], zc_ss)
-    bon_copy.wait()
-    for g in range(len(CHUNKS)):
-        put(g).wait()
+
+
+def write_out(*refs):
+    copies = [pltpu.make_async_copy(refs[k], refs[4 + k], refs[8].at[k]) for k in range(4)]
+    for c in copies:
+        c.start()
+    for c in copies:
+        c.wait()
 
 
 def solution(mesh):
@@ -368,26 +382,25 @@
                                                                                              LANES)
         xt = x_draft.T
         nunit = (nseq // LANES) * npos
-        any_ = pl.BlockSpec(memory_space=pl.ANY)
+        hbm = pl.BlockSpec(memory_space=pltpu.HBM)
         vmem = pl.BlockSpec(memory_space=pltpu.VMEM)
         dma, vm = pltpu.SemaphoreType.DMA, pltpu.VMEM
-        acc, exp, res, bonus = pl.pallas_call(
+        outs = pl.pallas_call(
             functools.partial(kernel, (na, nb)),
             out_shape=[
                 jax.ShapeDtypeStruct((ndraft, nseq), F32),
                 jax.ShapeDtypeStruct((1, nseq), F32),
-                jax.ShapeDtypeStruct((nd, per_src, nt * ndraft, LANES), F32),
+                jax.ShapeDtypeStruct((nseq * nt * ndraft, LANES), F32),
                 jax.ShapeDtypeStruct((nseq, vloc), F32),
             ],
-            in_specs=[any_, any_, any_, vmem],
-            out_specs=[vmem, vmem, any_, any_],
+            in_specs=[hbm] * 4,
+            out_specs=[vmem] * 4,
             scratch_shapes=[
                 vm((NBUF, ROWS, dm), jnp.bfloat16),
                 vm((dm, vloc), jnp.bfloat16),
+                vm((ndraft, nseq), jnp.int32),
                 vm((per_src, nd, 8, LANES), F32),
                 vm((nd, per_src, 8, LANES), F32),
-                vm((nseq * 8, LANES), F32),
-                vm((nseq, vloc), F32),
                 vm((ROWS, vloc), F32),
                 vm((nunit, 4, LANES), F32),
                 vm((nd, 4, LANES), F32),
@@ -402,9 +415,18 @@
                 dma, dma((len(CHUNKS) - 1,)), dma, dma,
             ],
             compiler_params=pltpu.CompilerParams(collective_id=0, has_side_effects=True,
-                                                 vmem_limit_bytes=48 * 1024 * 1024),
+                                                 vmem_limit_bytes=46 * 1024 * 1024),
             name="verify",
-        )(h5, w_head, q4, xt)
+        )(*[pltpu.with_memory_space_constraint(a, pltpu.HBM) for a in (h5, w_head, q4, xt)])
+        acc, exp, res, bonus = pl.pallas_call(
+            write_out,
+            out_shape=[jax.ShapeDtypeStruct(o.shape, o.dtype) for o in outs],
+            in_specs=[vmem] * 4,
+            out_specs=[hbm] * 4,
+            scratch_shapes=[dma((4,))],
+            compiler_params=pltpu.CompilerParams(vmem_limit_bytes=4 * 1024 * 1024),
+            name="write_out",
+        )(*outs)
         residual = res.reshape(nseq, nt, ndraft, LANES).transpose(0, 2, 1, 3).reshape(nseq, ndraft, vloc)
         return acc.T, exp.reshape(nseq), residual, bonus
 

time: 136 us -> 99.2 us (0.73)
  Pallas kernels: 126 us -> 98.5 us
  local copies, waits for them, and re-layouts: 9.39 us -> 0 us
    pallas_call x1, Pallas kernels: 126 us -> 96.1 us  [local_step(): pl.pallas_call(functools.partial(kernel, (na, nb)), out_shape=[jax.ShapeD...]
    unnamed x8 -> x0, local copies, waits for them, and re-layouts: 9.39 us -> none
    pallas_call x0 -> x1, Pallas kernels: none -> 2.4 us  [local_step(): pl.pallas_call(write_out, out_shape=[jax.ShapeDtypeStruct(o.shape, o.dtyp...]
where the time goes in v2:
time: 99.2 us; the launch traced here: 99.1 us
  Pallas kernels  98.5 us (99%)
    pallas_call x1, Pallas kernels, local_step(): pl.pallas_call(functools.partial(kernel, (na, nb)), out_shape=[jax.ShapeD...  96.1 us
    pallas_call x1, Pallas kernels, local_step(): pl.pallas_call(write_out, out_shape=[jax.ShapeDtypeStruct(o.shape, o.dtyp...  2.4 us

profile of v2, /device:TPU:1, one launch (start us, length us, event | category | flops | bytes accessed | tf_op | source)
XLA Modules:
  0.0 99.1 jit_solution(10082383615287149013)
XLA Ops:
  0.6 96.1 %verify.1 = (f32[4,1024]{1,0:T(4,128)S(1)}, f32[1,1024]{1,0:T(1,128)S(1)}, f32[8192,128]{1,0:T(8,128)S(1)}, f32[1024,256]{1,0:T(8,128)S(1)}) custom-call(bf16[5,1024,4096]{2,1,0:T(8,128)(2,1)} %bitcast.14, bf16[4096,256]{1,0:T(8,128)(2,1)} %w_ref.1, f32[8,128,8,128]{3,2,1,0:T(8,128)} %bitcast.15, s32[4,1024]{1,0:T(4,128)} %bitcast.16), custom_call_target="tpu_custom_call" | custom-call | tf_op jit(solution)/shard_map/verify/pallas_call | solution.py:388
  96.7 2.4 %write_out.1 = (f32[4,1024]{1,0:T(4,128)}, f32[1,1024]{1,0:T(1,128)}, f32[8192,128]{1,0:T(8,128)}, f32[1024,256]{1,0:T(8,128)}) custom-call(f32[4,1024]{1,0:T(4,128)S(1)} %get-tuple-element.12.refs_0_, f32[1,1024]{1,0:T(1,128)S(1)} %get-tuple-element.13.refs_1_, f32[8192,128]{1,0:T(8,128)S(1)} %get-tuple-element.14.refs_2_, ...), custom_call_target="tpu_custom_call" | custom-call | tf_op jit(solution)/shard_map/write_out/pallas_call | solution.py:421

commit v3 on v2

--- a/solution.py
+++ b/solution.py
@@ -12,7 +12,7 @@
 MESH = pl.DeviceIdType.MESH
 F32 = jnp.float32
 LANES = 128
-CHUNKS = ((0, 4), (4, 1), (5, 2), (7, 1))
+CHUNKS = ((0, 3), (3, 1), (4, 3), (7, 1))
 ROWS = 256
 NBUF = 3
 
@@ -41,18 +41,21 @@
     ys = [((py + k) % 4) * 4 for k in range(4)]
     cores = [me_a, (me_a + 1) % na]
 
-    def each_peer(fn):
+    def each_peer(fn, far=False):
+        first = 2 if far else 0
+
         def plane(kz, carry):
-            zz = pz + kz
+            zz = pz + kz + first
+            zz = jnp.where(zz >= 4, zz - 4, zz)
             base = jnp.where(zz >= 4, zz - 4, zz) * 16
-            for ky in range(4):
-                for kx in (1, 3, 2, 0):
+            for ky in (2, 1, 3, 0) if far else range(4):
+                for kx in (2, 1, 3, 0) if far else (1, 3, 2, 0):
                     for ka in range(na):
                         b = base + ys[ky] + xs[kx]
                         f = cores[ka] * nb + b
                         ident = {"tpa": cores[ka], "tpb": b}
                         if ka == kx == ky == 0:
-                            @pl.when(kz > 0)
+                            @pl.when(kz != (4 - first) % 4)
                             def _():
                                 fn(f, ident)
                         else:
@@ -91,7 +94,7 @@
         h_copy(t).start()
 
     barrier = pltpu.get_barrier_semaphore()
-    each_peer(lambda f, ident: pl.semaphore_signal(barrier, inc=1, device_id=ident, device_id_type=MESH))
+    each_peer(lambda f, ident: pl.semaphore_signal(barrier, inc=1, device_id=ident, device_id_type=MESH), far=True)
     q_copy.wait()
 
     def local_bulk(g):
@@ -100,26 +103,6 @@
 
     for g in range(len(CHUNKS)):
         local_bulk(g).start()
-    pl.semaphore_wait(barrier, nd - 1)
-
-    def send_bulk(g):
-        c0, n = CHUNKS[g]
-
-        def one(c, carry):
-            each_peer(lambda f, ident: pltpu.make_async_remote_copy(
-                src_ref=qsrc.at[c, f], dst_ref=qdst.at[me, c], send_sem=bulk_ss.at[g], recv_sem=bulk_rs.at[g],
-                device_id=ident, device_id_type=MESH).start())
-            return carry
-
-        lax.fori_loop(c0, c0 + n, one, 0)
-
-    def wait_bulk(g):
-        c0, n = CHUNKS[g]
-        ref = qdst.at[:, pl.ds(c0, n)]
-        pltpu.make_async_copy(ref, ref, bulk_rs.at[g]).wait()
-
-    send_bulk(0)
-
     x_copy.wait()
     xb = x_ref[:, pl.ds(pl.multiple_of((me // 16) * LANES, LANES), LANES)].astype(F32)
     targets = []
@@ -137,6 +120,26 @@
     for c in range(per_src):
         col = jnp.sum(accs[c], axis=1, keepdims=True)
         qp = jnp.where(lane[:4] == (me % 16) * per_src + c, col[:4] + col[4:], qp)
+
+    pl.semaphore_wait(barrier, nd - 1)
+
+    def send_bulk(g):
+        c0, n = CHUNKS[g]
+
+        def one(c, carry):
+            each_peer(lambda f, ident: pltpu.make_async_remote_copy(
+                src_ref=qsrc.at[c, f], dst_ref=qdst.at[me, c], send_sem=bulk_ss.at[g], recv_sem=bulk_rs.at[g],
+                device_id=ident, device_id_type=MESH).start())
+            return carry
+
+        lax.fori_loop(c0, c0 + n, one, 0)
+
+    def wait_bulk(g):
+        c0, n = CHUNKS[g]
+        ref = qdst.at[:, pl.ds(c0, n)]
+        pltpu.make_async_copy(ref, ref, bulk_rs.at[g]).wait()
+
+    send_bulk(0)
 
     w_copy.wait()
     my_base = (me * vloc).astype(F32)
@@ -212,17 +215,27 @@
         pltpu.make_async_copy(ag_send, ag_recv.at[my_unit], ag_rs).start()
         each_peer(lambda f, ident: pltpu.make_async_remote_copy(
             src_ref=ag_send, dst_ref=ag_recv.at[my_unit], send_sem=ag_ss, recv_sem=ag_rs, device_id=ident,
-            device_id_type=MESH).start())
+            device_id_type=MESH).start(), far=True)
 
     send_bulk(2)
 
     pltpu.make_async_copy(ag_recv, ag_recv, ag_rs).wait()
 
-    def probs(blk, carry):
-        def rows(k):
-            return jnp.concatenate([ag_recv[blk * npos + i, k:k + 1, :] for i in range(ndraft)], axis=0)
-
-        m8, r8, a4 = twice(rows(0)), twice(rows(1)), rows(2)
+    def stat_rows(blk, k):
+        return jnp.concatenate([ag_recv[blk * npos + i, k:k + 1, :] for i in range(ndraft)], axis=0)
+
+    def probs(c0, n):
+        def body(blk, carry):
+            m8, r8 = twice(stat_rows(blk, 0)), twice(stat_rows(blk, 1))
+            for j in range(LANES):
+                if c0 <= j % per_src < c0 + n:
+                    at = pl.ds(pl.multiple_of((blk * LANES + j) * 8, 8), 8)
+                    zr[at, :] = jnp.exp(zr[at, :] - m8[:, j:j + 1]) * r8[:, j:j + 1]
+            return carry
+        lax.fori_loop(0, nblk, body, 0)
+
+    def verdicts(blk, carry):
+        a4 = stat_rows(blk, 2)
         cols = pl.ds(pl.multiple_of(blk * LANES, LANES), LANES)
         acc_ref[:, cols] = a4
         run, tot = a4[0:1], a4[0:1]
@@ -230,14 +243,9 @@
             run = run * a4[i:i + 1]
             tot = tot + run
         exp_ref[:, cols] = tot
-        for j in range(LANES):
-            at = pl.ds(pl.multiple_of((blk * LANES + j) * 8, 8), 8)
-            zr[at, :] = jnp.exp(zr[at, :] - m8[:, j:j + 1]) * r8[:, j:j + 1]
         u4 = blk * npos + ndraft
         z4[cols, :] = jnp.exp(z4[cols, :] - to_col(ag_recv[u4, 0:1, :])) * to_col(ag_recv[u4, 1:2, :])
         return carry
-
-    lax.fori_loop(0, nblk, probs, 0)
 
     def excess(g):
         c0, n = CHUNKS[g]
@@ -280,7 +288,7 @@
                 pltpu.make_async_copy(za_send, za_recv.at[c], za_rs.at[g]).start()
                 each_peer(lambda f, ident: pltpu.make_async_remote_copy(
                     src_ref=za_send, dst_ref=za_recv.at[c], send_sem=za_ss, recv_sem=za_rs.at[g], device_id=ident,
-                    device_id_type=MESH).start())
+                    device_id_type=MESH).start(), far=True)
 
     def wait_sums(g):
         c0, n = CHUNKS[g]
@@ -303,16 +311,20 @@
         lax.fori_loop(c0, c0 + n, one, 0)
 
     last = len(CHUNKS) - 1
+    half = CHUNKS[2][0]
+    probs(0, half)
     for g in range(2):
         wait_bulk(g)
         excess(g)
         send_sums(g)
     send_bulk(3)
+    probs(half, per_src - half)
     for g in range(2):
         own_sums(g)
     wait_bulk(2)
     excess(2)
     send_sums(2)
+    lax.fori_loop(0, nblk, verdicts, 0)
     own_sums(2)
     for g in range(2):
         wait_sums(g)
@@ -323,7 +335,7 @@
     pltpu.make_async_copy(zs_send.at[c_last], zb_recv.at[me], zc_rs).start()
     each_peer(lambda f, ident: pltpu.make_async_remote_copy(
         src_ref=zs_send.at[c_last], dst_ref=zb_recv.at[me], send_sem=zc_ss, recv_sem=zc_rs, device_id=ident,
-        device_id_type=MESH).start())
+        device_id_type=MESH).start(), far=True)
     wait_sums(2)
     finish(2)
     pltpu.make_async_copy(zb_recv, zb_recv, zc_rs).wait()

time: 99.2 us -> 89.9 us (0.906)
  Pallas kernels: 98.5 us -> 89.2 us
    pallas_call x1, Pallas kernels: 96.1 us -> 86.8 us  [local_step(): pl.pallas_call(functools.partial(kernel, (na, nb)), out_shape=[jax.ShapeD...]
where the time goes in v3:
time: 89.9 us; the launch traced here: 89.8 us
  Pallas kernels  89.2 us (99%)
    pallas_call x1, Pallas kernels, local_step(): pl.pallas_call(functools.partial(kernel, (na, nb)), out_shape=[jax.ShapeD...  86.8 us
    pallas_call x1, Pallas kernels, local_step(): pl.pallas_call(write_out, out_shape=[jax.ShapeDtypeStruct(o.shape, o.dtyp...  2.4 us

profile of v3, /device:TPU:1, one launch (start us, length us, event | category | flops | bytes accessed | tf_op | source)
XLA Modules:
  0.0 89.8 jit_solution(2776521434071767326)
XLA Ops:
  0.6 86.8 %verify.1 = (f32[4,1024]{1,0:T(4,128)S(1)}, f32[1,1024]{1,0:T(1,128)S(1)}, f32[8192,128]{1,0:T(8,128)S(1)}, f32[1024,256]{1,0:T(8,128)S(1)}) custom-call(bf16[5,1024,4096]{2,1,0:T(8,128)(2,1)} %bitcast.14, bf16[4096,256]{1,0:T(8,128)(2,1)} %w_ref.1, f32[8,128,8,128]{3,2,1,0:T(8,128)} %bitcast.15, s32[4,1024]{1,0:T(4,128)} %bitcast.16), custom_call_target="tpu_custom_call" | custom-call | tf_op jit(solution)/shard_map/verify/pallas_call | solution.py:400
  87.4 2.4 %write_out.1 = (f32[4,1024]{1,0:T(4,128)}, f32[1,1024]{1,0:T(1,128)}, f32[8192,128]{1,0:T(8,128)}, f32[1024,256]{1,0:T(8,128)}) custom-call(f32[4,1024]{1,0:T(4,128)S(1)} %get-tuple-element.12.refs_0_, f32[1,1024]{1,0:T(1,128)S(1)} %get-tuple-element.13.refs_1_, f32[8192,128]{1,0:T(8,128)S(1)} %get-tuple-element.14.refs_2_, ...), custom_call_target="tpu_custom_call" | custom-call | tf_op jit(solution)/shard_map/write_out/pallas_call | solution.py:433

commit v4 on v3

--- a/solution.py
+++ b/solution.py
@@ -12,15 +12,15 @@
 MESH = pl.DeviceIdType.MESH
 F32 = jnp.float32
 LANES = 128
-CHUNKS = ((0, 3), (3, 1), (4, 3), (7, 1))
+CHUNKS = ((0, 3), (3, 1), (4, 2), (6, 1), (7, 1))
 ROWS = 256
 NBUF = 3
-
-
-def kernel(dims, h_ref, w_ref, q_ref, xin_ref, acc_ref, exp_ref, zr, z4,
-           hbuf, wbuf, x_ref, qsrc, qdst, zb, st_send, st_recv, ag_send, ag_recv, zs_send, zs_recv, za_send, za_recv,
-           zb_recv, h_sem, w_sem, q_sem, x_sem, bulk_ss, bulk_rs, st_ss, st_rs, ag_ss, ag_rs, zs_ss, zs_rs, za_ss,
-           za_rs, zc_ss, zc_rs):
+EARLY = 3
+
+
+def kernel(dims, h_ref, w_ref, q_ref, xin_ref, acc_ref, exp_ref, zr, z4, rz_ref,
+           hbuf, wbuf, x_ref, qsrc, qdst, zb, st_send, st_recv, ag_send, ag_recv, zs_send, zs_recv, h_sem, w_sem, q_sem,
+           x_sem, bulk_ss, bulk_rs, st_ss, st_rs, ag_ss, ag_rs, zs_ss, zs_rs):
     na, nb = dims
     nd = na * nb
     me_a, me_b = lax.axis_index("tpa"), lax.axis_index("tpb")
@@ -115,13 +115,13 @@
         base = (d * vloc).astype(F32)
         return tuple(a + jnp.where(t == base, qsrc[c, d], 0.0) for c, (a, t) in enumerate(zip(accs, targets)))
 
-    accs = lax.fori_loop(0, nd, pick_q, tuple(jnp.zeros((8, LANES), F32) for _ in range(per_src)))
+    accs = lax.fori_loop(0, nd, pick_q, tuple(jnp.zeros((8, LANES), F32) for _ in range(per_src)),
+                         unroll=8)
     qp = jnp.zeros((4, LANES), F32)
     for c in range(per_src):
         col = jnp.sum(accs[c], axis=1, keepdims=True)
         qp = jnp.where(lane[:4] == (me % 16) * per_src + c, col[:4] + col[4:], qp)
 
-    pl.semaphore_wait(barrier, nd - 1)
 
     def send_bulk(g):
         c0, n = CHUNKS[g]
@@ -138,8 +138,6 @@
         c0, n = CHUNKS[g]
         ref = qdst.at[:, pl.ds(c0, n)]
         pltpu.make_async_copy(ref, ref, bulk_rs.at[g]).wait()
-
-    send_bulk(0)
 
     w_copy.wait()
     my_base = (me * vloc).astype(F32)
@@ -177,7 +175,10 @@
                 z4[pl.ds(pl.multiple_of(blk * LANES, LANES), LANES), :] = zz
         return carry
 
-    lax.fori_loop(0, npos * per_pos, matmul, 0)
+    lax.fori_loop(0, EARLY, matmul, 0)
+    pl.semaphore_wait(barrier, nd - 1)
+    send_bulk(0)
+    lax.fori_loop(EARLY, npos * per_pos, matmul, 0)
 
     def owner(u):
         return u * 3
@@ -217,7 +218,8 @@
             src_ref=ag_send, dst_ref=ag_recv.at[my_unit], send_sem=ag_ss, recv_sem=ag_rs, device_id=ident,
             device_id_type=MESH).start(), far=True)
 
-    send_bulk(2)
+    for g in range(2, len(CHUNKS)):
+        send_bulk(g)
 
     pltpu.make_async_copy(ag_recv, ag_recv, ag_rs).wait()
 
@@ -261,85 +263,39 @@
 
         accs = lax.fori_loop(0, nd, body, tuple(jnp.zeros((8, LANES), F32) for _ in range(n)), unroll=4)
         for c in range(n):
-            zs_send[c0 + c] = accs[c][:4] + accs[c][4:]
-
-    def z_owner(c):
-        return (c * 16 + 5) % nd
-
-    def send_sums(g):
-        c0, n = CHUNKS[g]
-        for c in range(c0, c0 + n):
-            @pl.when(me != z_owner(c))
-            def _():
-                pltpu.make_async_remote_copy(src_ref=zs_send.at[c], dst_ref=zs_recv.at[me], send_sem=zs_ss,
-                                             recv_sem=zs_rs, device_id=dev(z_owner(c)), device_id_type=MESH).start()
-
-    def sum_of(ref):
-        return lax.fori_loop(0, nd, lambda s, a: a + ref[s], jnp.zeros((4, LANES), F32), unroll=8)
-
-    def own_sums(g):
-        c0, n = CHUNKS[g]
-        for c in range(c0, c0 + n):
-            @pl.when(me == z_owner(c))
-            def _():
-                pltpu.make_async_copy(zs_send.at[c], zs_recv.at[me], zs_rs).start()
-                pltpu.make_async_copy(zs_recv, zs_recv, zs_rs).wait()
-                za_send[...] = sum_of(zs_recv)
-                pltpu.make_async_copy(za_send, za_recv.at[c], za_rs.at[g]).start()
-                each_peer(lambda f, ident: pltpu.make_async_remote_copy(
-                    src_ref=za_send, dst_ref=za_recv.at[c], send_sem=za_ss, recv_sem=za_rs.at[g], device_id=ident,
-                    device_id_type=MESH).start(), far=True)
-
-    def wait_sums(g):
-        c0, n = CHUNKS[g]
-        ref = za_recv.at[pl.ds(c0, n)]
-        pltpu.make_async_copy(ref, ref, za_rs.at[g]).wait()
-
-    def scale(c, tile):
-        r8 = twice(1.0 / tile)
-        for s in range(nd):
-            at = pl.ds((s * per_src + c) * 8, 8)
-            zr[at, :] = zr[at, :] * r8[:, s:s + 1]
-
-    def finish(g):
-        c0, n = CHUNKS[g]
-
-        def one(c, carry):
-            scale(c, za_recv[c])
-            return carry
-
-        lax.fori_loop(c0, c0 + n, one, 0)
-
-    last = len(CHUNKS) - 1
+            part = accs[c][:4] + accs[c][4:]
+            zs_send[0, (c0 + c) // 2, ((c0 + c) % 2) * 4:((c0 + c) % 2) * 4 + 4] = part
+
     half = CHUNKS[2][0]
     probs(0, half)
     for g in range(2):
         wait_bulk(g)
         excess(g)
-        send_sums(g)
-    send_bulk(3)
     probs(half, per_src - half)
-    for g in range(2):
-        own_sums(g)
-    wait_bulk(2)
-    excess(2)
-    send_sums(2)
     lax.fori_loop(0, nblk, verdicts, 0)
-    own_sums(2)
-    for g in range(2):
-        wait_sums(g)
-        finish(g)
-    wait_bulk(last)
-    excess(last)
-    c_last = CHUNKS[last][0]
-    pltpu.make_async_copy(zs_send.at[c_last], zb_recv.at[me], zc_rs).start()
-    each_peer(lambda f, ident: pltpu.make_async_remote_copy(
-        src_ref=zs_send.at[c_last], dst_ref=zb_recv.at[me], send_sem=zc_ss, recv_sem=zc_rs, device_id=ident,
-        device_id_type=MESH).start(), far=True)
-    wait_sums(2)
-    finish(2)
-    pltpu.make_async_copy(zb_recv, zb_recv, zc_rs).wait()
-    scale(c_last, sum_of(zb_recv))
+    for g in range(2, len(CHUNKS)):
+        wait_bulk(g)
+        excess(g)
+
+    axes = [[{"tpa": cores[1], "tpb": me_b}],
+            [{"tpa": me_a, "tpb": me_b - px + xs[k]} for k in (2, 1, 3)],
+            [{"tpa": me_a, "tpb": me_b - py * 4 + ys[k]} for k in (2, 1, 3)],
+            [{"tpa": me_a, "tpb": me_b - pz * 16 + ((pz + k) % 4) * 16} for k in (2, 1, 3)]]
+    first = 0
+    for t, group in enumerate(axes):
+        for k, ident in enumerate(group):
+            pltpu.make_async_remote_copy(src_ref=zs_send.at[t], dst_ref=zs_recv.at[first + k], send_sem=zs_ss.at[t],
+                                         recv_sem=zs_rs.at[t], device_id=ident, device_id_type=MESH).start()
+        ref = zs_recv.at[pl.ds(first, len(group))]
+        pltpu.make_async_copy(ref, ref, zs_rs.at[t]).wait()
+        total = zs_send[t]
+        for k in range(len(group)):
+            total = total + zs_recv[first + k]
+        if t + 1 < len(axes):
+            zs_send[t + 1] = total
+        else:
+            rz_ref[...] = 1.0 / total
+        first += len(group)
 
     def drain(ref, sem):
         pltpu.make_async_copy(ref, ref, sem).wait()
@@ -356,26 +312,29 @@
     def _():
         drain(st_send, st_ss)
 
-    nz = c_last
-    is_zowner = (me % 16 == 5) & (me // 16 < nz)
-
-    @pl.when(is_zowner)
-    def _():
-        drain(zs_send.at[pl.ds(0, nz - 1)], zs_ss)
-        drain(st_recv.at[pl.ds(0, nd - 1)], za_ss)
-
-    @pl.when(jnp.logical_not(is_zowner))
-    def _():
-        drain(zs_send.at[pl.ds(0, nz)], zs_ss)
-
-    drain(st_recv.at[pl.ds(0, nd - 1)], zc_ss)
-
-
-def write_out(*refs):
-    copies = [pltpu.make_async_copy(refs[k], refs[4 + k], refs[8].at[k]) for k in range(4)]
-    for c in copies:
+    for t, group in enumerate(axes):
+        drain(zs_recv.at[pl.ds(0, len(group))], zs_ss.at[t])
+
+
+def write_out(acc_ref, exp_ref, num_ref, bon_ref, rz_ref, acc_out, exp_out, res_out, bon_out, res, sem):
+    nd, per_src = num_ref.shape[:2]
+    small = [pltpu.make_async_copy(a, b, sem.at[k]) for k, (a, b) in enumerate(
+        ((acc_ref, acc_out), (exp_ref, exp_out), (bon_ref, bon_out)))]
+    for c in small:
         c.start()
-    for c in copies:
+
+    def put(c):
+        return pltpu.make_async_copy(res.at[:, c], res_out.at[:, c], sem.at[3 + c])
+
+    for c in range(per_src):
+        tile = rz_ref[c // 2, (c % 2) * 4:(c % 2) * 4 + 4]
+        r8 = jnp.concatenate([tile, tile], axis=0)
+        for s in range(nd):
+            res[s, c] = num_ref[s, c] * r8[:, s:s + 1]
+        put(c).start()
+    for c in range(per_src):
+        put(c).wait()
+    for c in small:
         c.wait()
 
 
@@ -404,9 +363,10 @@
                 jax.ShapeDtypeStruct((1, nseq), F32),
                 jax.ShapeDtypeStruct((nseq * nt * ndraft, LANES), F32),
                 jax.ShapeDtypeStruct((nseq, vloc), F32),
+                jax.ShapeDtypeStruct((per_src // 2, 8, LANES), F32),
             ],
             in_specs=[hbm] * 4,
-            out_specs=[vmem] * 4,
+            out_specs=[vmem] * 5,
             scratch_shapes=[
                 vm((NBUF, ROWS, dm), jnp.bfloat16),
                 vm((dm, vloc), jnp.bfloat16),
@@ -418,27 +378,27 @@
                 vm((nd, 4, LANES), F32),
                 vm((4, LANES), F32),
                 vm((nunit, 4, LANES), F32),
-                vm((per_src, 4, LANES), F32),
-                vm((nd, 4, LANES), F32),
-                vm((4, LANES), F32),
-                vm((per_src, 4, LANES), F32),
-                vm((nd, 4, LANES), F32),
-                dma((NBUF,)), dma, dma, dma, dma((len(CHUNKS),)), dma((len(CHUNKS),)), dma, dma, dma, dma, dma, dma,
-                dma, dma((len(CHUNKS) - 1,)), dma, dma,
+                vm((4, per_src // 2, 8, LANES), F32),
+                vm((10, per_src // 2, 8, LANES), F32),
+                dma((NBUF,)), dma, dma, dma, dma((len(CHUNKS),)), dma((len(CHUNKS),)), dma, dma, dma, dma, dma((4,)),
+                dma((4,)),
             ],
             compiler_params=pltpu.CompilerParams(collective_id=0, has_side_effects=True,
                                                  vmem_limit_bytes=46 * 1024 * 1024),
             name="verify",
         )(*[pltpu.with_memory_space_constraint(a, pltpu.HBM) for a in (h5, w_head, q4, xt)])
+        acc, exp, num, bonus, rz = outs
+        num = num.reshape(nd, per_src, nt * ndraft, LANES)
+        outs = (acc, exp, num, bonus)
         acc, exp, res, bonus = pl.pallas_call(
             write_out,
             out_shape=[jax.ShapeDtypeStruct(o.shape, o.dtype) for o in outs],
-            in_specs=[vmem] * 4,
+            in_specs=[vmem] * 5,
             out_specs=[hbm] * 4,
-            scratch_shapes=[dma((4,))],
-            compiler_params=pltpu.CompilerParams(vmem_limit_bytes=4 * 1024 * 1024),
+            scratch_shapes=[vm(num.shape, F32), dma((3 + per_src,))],
+            compiler_params=pltpu.CompilerParams(vmem_limit_bytes=8 * 1024 * 1024),
             name="write_out",
-        )(*outs)
+        )(*outs, rz)
         residual = res.reshape(nseq, nt, ndraft, LANES).transpose(0, 2, 1, 3).reshape(nseq, ndraft, vloc)
         return acc.T, exp.reshape(nseq), residual, bonus
 

time: 89.9 us -> 89.9 us (level); the launches traced: 89.8 us -> 88.5 us
  Pallas kernels: 89.2 us -> 87.9 us
    pallas_call x1, Pallas kernels: 86.8 us -> 84.7 us  [local_step(): pl.pallas_call(functools.partial(kernel, (na, nb)), out_shape=[jax.ShapeD...]
where the time goes in v4:
time: 89.9 us; the launch traced here: 88.5 us
  Pallas kernels  87.9 us (98%)
    pallas_call x1, Pallas kernels, local_step(): pl.pallas_call(functools.partial(kernel, (na, nb)), out_shape=[jax.ShapeD...  84.7 us
    pallas_call x1, Pallas kernels, local_step(): pl.pallas_call(write_out, out_shape=[jax.ShapeDtypeStruct(o.shape, o.dtyp...  3.16 us

profile of v4, /device:TPU:1, one launch (start us, length us, event | category | flops | bytes accessed | tf_op | source)
XLA Modules:
  0.0 88.5 jit_solution(15553723355524848027)
XLA Ops:
  0.6 84.7 %verify.1 = (f32[4,1024]{1,0:T(4,128)S(1)}, f32[1,1024]{1,0:T(1,128)S(1)}, f32[8192,128]{1,0:T(8,128)S(1)}, f32[1024,256]{1,0:T(8,128)S(1)}, f32[4,8,128]{2,1,0:T(8,128)S(1)}) custom-call(bf16[5,1024,4096]{2,1,0:T(8,128)(2,1)} %bitcast.16, bf16[4096,256]{1,0:T(8,128)(2,1)} %w_ref.1, f32[8,128,8,128]{3,2,1,0:T(8,128)} %bitcast.17, s32[4,1024]{1,0:T(4,128)} %bitcast.18), custom_call_target="tpu_custom_call" | custom-call | tf_op jit(solution)/shard_map/verify/pallas_call | solution.py:359
  85.4 3.2 %write_out.1 = (f32[4,1024]{1,0:T(4,128)}, f32[1,1024]{1,0:T(1,128)}, f32[128,8,8,128]{3,2,1,0:T(8,128)}, f32[1024,256]{1,0:T(8,128)}) custom-call(f32[4,1024]{1,0:T(4,128)S(1)} %get-tuple-element.13.acc_ref, f32[1,1024]{1,0:T(1,128)S(1)} %get-tuple-element.14.exp_ref, f32[128,8,8,128]{3,2,1,0:T(8,128)S(1)} %bitcast.15, ...), custom_call_target="tpu_custom_call" | custom-call | tf_op jit(solution)/shard_map/write_out/pallas_call | solution.py:393

commit v5 on v4

--- a/solution.py
+++ b/solution.py
@@ -12,7 +12,7 @@
 MESH = pl.DeviceIdType.MESH
 F32 = jnp.float32
 LANES = 128
-CHUNKS = ((0, 3), (3, 1), (4, 2), (6, 1), (7, 1))
+CHUNKS = ((0, 3), (3, 2), (5, 1), (6, 1), (7, 1))
 ROWS = 256
 NBUF = 3
 EARLY = 3
@@ -202,7 +202,7 @@
     def _():
         pltpu.make_async_copy(st_send.at[my_unit], st_recv.at[me], st_rs).start()
         pltpu.make_async_copy(st_recv, st_recv, st_rs).wait()
-        mx = lax.fori_loop(0, nd, lambda s, m: jnp.maximum(m, st_recv[s]), st_recv[0])[0:1]
+        mx = lax.fori_loop(0, nd, lambda s, m: jnp.maximum(m, st_recv[s]), st_recv[0], unroll=8)[0:1]
 
         def add(s, carry):
             t = st_recv[s]
@@ -210,7 +210,7 @@
             return es + jnp.exp(t[0:1] - mx) * t[1:2], zp + t[2:3], qq + t[3:4]
 
         zero = jnp.zeros((1, LANES), F32)
-        es, zp, qq = lax.fori_loop(0, nd, add, (zero, zero, zero))
+        es, zp, qq = lax.fori_loop(0, nd, add, (zero, zero, zero), unroll=8)
         accept = jnp.minimum(1.0, jnp.exp(zp - mx) / es / qq)
         ag_send[...] = jnp.where(sub4 == 0, mx, jnp.where(sub4 == 1, 1.0 / es, accept))
         pltpu.make_async_copy(ag_send, ag_recv.at[my_unit], ag_rs).start()
@@ -272,13 +272,11 @@
         wait_bulk(g)
         excess(g)
     probs(half, per_src - half)
-    lax.fori_loop(0, nblk, verdicts, 0)
     for g in range(2, len(CHUNKS)):
         wait_bulk(g)
         excess(g)
 
-    axes = [[{"tpa": cores[1], "tpb": me_b}],
-            [{"tpa": me_a, "tpb": me_b - px + xs[k]} for k in (2, 1, 3)],
+    axes = [[{"tpa": cores[a], "tpb": me_b - px + xs[k]} for k in (2, 1, 3, 0) for a in range(na) if (k, a) != (0, 0)],
             [{"tpa": me_a, "tpb": me_b - py * 4 + ys[k]} for k in (2, 1, 3)],
             [{"tpa": me_a, "tpb": me_b - pz * 16 + ((pz + k) % 4) * 16} for k in (2, 1, 3)]]
     first = 0
@@ -286,6 +284,8 @@
         for k, ident in enumerate(group):
             pltpu.make_async_remote_copy(src_ref=zs_send.at[t], dst_ref=zs_recv.at[first + k], send_sem=zs_ss.at[t],
                                          recv_sem=zs_rs.at[t], device_id=ident, device_id_type=MESH).start()
+        if t == 0:
+            lax.fori_loop(0, nblk, verdicts, 0)
         ref = zs_recv.at[pl.ds(first, len(group))]
         pltpu.make_async_copy(ref, ref, zs_rs.at[t]).wait()
         total = zs_send[t]
@@ -378,10 +378,10 @@
                 vm((nd, 4, LANES), F32),
                 vm((4, LANES), F32),
                 vm((nunit, 4, LANES), F32),
-                vm((4, per_src // 2, 8, LANES), F32),
-                vm((10, per_src // 2, 8, LANES), F32),
-                dma((NBUF,)), dma, dma, dma, dma((len(CHUNKS),)), dma((len(CHUNKS),)), dma, dma, dma, dma, dma((4,)),
-                dma((4,)),
+                vm((3, per_src // 2, 8, LANES), F32),
+                vm((13, per_src // 2, 8, LANES), F32),
+                dma((NBUF,)), dma, dma, dma, dma((len(CHUNKS),)), dma((len(CHUNKS),)), dma, dma, dma, dma, dma((3,)),
+                dma((3,)),
             ],
             compiler_params=pltpu.CompilerParams(collective_id=0, has_side_effects=True,
                                                  vmem_limit_bytes=46 * 1024 * 1024),

time: 89.9 us -> 100 us (1.11); the launches traced: 88.5 us -> 99.9 us
  Pallas kernels: 87.9 us -> 99.3 us
    pallas_call x1, Pallas kernels: 84.7 us -> 96.1 us  [local_step(): pl.pallas_call(functools.partial(kernel, (na, nb)), out_shape=[jax.ShapeD...]
where the time goes in v5:
time: 100 us; the launch traced here: 99.9 us
  Pallas kernels  99.3 us (99%)
    pallas_call x1, Pallas kernels, local_step(): pl.pallas_call(functools.partial(kernel, (na, nb)), out_shape=[jax.ShapeD...  96.1 us
    pallas_call x1, Pallas kernels, local_step(): pl.pallas_call(write_out, out_shape=[jax.ShapeDtypeStruct(o.shape, o.dtyp...  3.16 us

profile of v5, /device:TPU:1, one launch (start us, length us, event | category | flops | bytes accessed | tf_op | source)
XLA Modules:
  0.0 99.9 jit_solution(5202342532001029924)
XLA Ops:
  0.6 96.1 %verify.1 = (f32[4,1024]{1,0:T(4,128)S(1)}, f32[1,1024]{1,0:T(1,128)S(1)}, f32[8192,128]{1,0:T(8,128)S(1)}, f32[1024,256]{1,0:T(8,128)S(1)}, f32[4,8,128]{2,1,0:T(8,128)S(1)}) custom-call(bf16[5,1024,4096]{2,1,0:T(8,128)(2,1)} %bitcast.16, bf16[4096,256]{1,0:T(8,128)(2,1)} %w_ref.1, f32[8,128,8,128]{3,2,1,0:T(8,128)} %bitcast.17, s32[4,1024]{1,0:T(4,128)} %bitcast.18), custom_call_target="tpu_custom_call" | custom-call | tf_op jit(solution)/shard_map/verify/pallas_call | solution.py:359
  96.7 3.2 %write_out.1 = (f32[4,1024]{1,0:T(4,128)}, f32[1,1024]{1,0:T(1,128)}, f32[128,8,8,128]{3,2,1,0:T(8,128)}, f32[1024,256]{1,0:T(8,128)}) custom-call(f32[4,1024]{1,0:T(4,128)S(1)} %get-tuple-element.13.acc_ref, f32[1,1024]{1,0:T(1,128)S(1)} %get-tuple-element.14.exp_ref, f32[128,8,8,128]{3,2,1,0:T(8,128)S(1)} %bitcast.15, ...), custom_call_target="tpu_custom_call" | custom-call | tf_op jit(solution)/shard_map/write_out/pallas_call | solution.py:393

commit v6 on v5

--- a/solution.py
+++ b/solution.py
@@ -12,7 +12,7 @@
 MESH = pl.DeviceIdType.MESH
 F32 = jnp.float32
 LANES = 128
-CHUNKS = ((0, 3), (3, 2), (5, 1), (6, 1), (7, 1))
+CHUNKS = ((0, 3), (3, 1), (4, 1), (5, 2), (7, 1))
 ROWS = 256
 NBUF = 3
 EARLY = 3
@@ -41,7 +41,7 @@
     ys = [((py + k) % 4) * 4 for k in range(4)]
     cores = [me_a, (me_a + 1) % na]
 
-    def each_peer(fn, far=False):
+    def each_peer(fn, far=False, own_core=False):
         first = 2 if far else 0
 
         def plane(kz, carry):
@@ -50,7 +50,7 @@
             base = jnp.where(zz >= 4, zz - 4, zz) * 16
             for ky in (2, 1, 3, 0) if far else range(4):
                 for kx in (2, 1, 3, 0) if far else (1, 3, 2, 0):
-                    for ka in range(na):
+                    for ka in range(1 if own_core else na):
                         b = base + ys[ky] + xs[kx]
                         f = cores[ka] * nb + b
                         ident = {"tpa": cores[ka], "tpb": b}
@@ -180,19 +180,17 @@
     send_bulk(0)
     lax.fori_loop(EARLY, npos * per_pos, matmul, 0)
 
-    def owner(u):
-        return u * 3
-
-    is_owner = (me % 3 == 0) & (me < nunit * 3)
-    my_unit = me // 3
+    my_unit = (me_b * 43) % nb
+    is_owner = my_unit < nunit
 
     def send_stats(u, carry):
-        f = owner(u)
-
-        @pl.when(f != me)
-        def _():
-            pltpu.make_async_remote_copy(src_ref=st_send.at[u], dst_ref=st_recv.at[me], send_sem=st_ss, recv_sem=st_rs,
-                                         device_id=dev(f), device_id_type=MESH).start()
+        chip = (u * 3) % nb
+        for a in range(na):
+            @pl.when((chip != me_b) | (me_a != a))
+            def _():
+                pltpu.make_async_remote_copy(src_ref=st_send.at[u], dst_ref=st_recv.at[me], send_sem=st_ss,
+                                             recv_sem=st_rs, device_id={"tpa": a, "tpb": chip},
+                                             device_id_type=MESH).start()
         return carry
 
     lax.fori_loop(0, nunit, send_stats, 0)
@@ -216,12 +214,13 @@
         pltpu.make_async_copy(ag_send, ag_recv.at[my_unit], ag_rs).start()
         each_peer(lambda f, ident: pltpu.make_async_remote_copy(
             src_ref=ag_send, dst_ref=ag_recv.at[my_unit], send_sem=ag_ss, recv_sem=ag_rs, device_id=ident,
-            device_id_type=MESH).start(), far=True)
-
-    for g in range(2, len(CHUNKS)):
+            device_id_type=MESH).start(), far=True, own_core=True)
+
+    send_bulk(2)
+
+    pltpu.make_async_copy(ag_recv, ag_recv, ag_rs).wait()
+    for g in range(3, len(CHUNKS)):
         send_bulk(g)
-
-    pltpu.make_async_copy(ag_recv, ag_recv, ag_rs).wait()
 
     def stat_rows(blk, k):
         return jnp.concatenate([ag_recv[blk * npos + i, k:k + 1, :] for i in range(ndraft)], axis=0)
@@ -305,11 +304,13 @@
 
     @pl.when(is_owner)
     def _():
+        drain(st_send, st_ss)
         drain(st_send.at[pl.ds(0, nunit - 1)], st_ss)
-        drain(st_recv.at[pl.ds(0, nd - 1)], ag_ss)
+        drain(st_recv.at[pl.ds(0, nb - 1)], ag_ss)
 
     @pl.when(jnp.logical_not(is_owner))
     def _():
+        drain(st_send, st_ss)
         drain(st_send, st_ss)
 
     for t, group in enumerate(axes):

time: 100 us -> 88.4 us (0.88)
  Pallas kernels: 99.3 us -> 87.2 us
    pallas_call x1, Pallas kernels: 96.1 us -> 84 us  [local_step(): pl.pallas_call(functools.partial(kernel, (na, nb)), out_shape=[jax.ShapeD...]
where the time goes in v6:
time: 88.4 us; the launch traced here: 87.8 us
  Pallas kernels  87.2 us (99%)
    pallas_call x1, Pallas kernels, local_step(): pl.pallas_call(functools.partial(kernel, (na, nb)), out_shape=[jax.ShapeD...  84 us
    pallas_call x1, Pallas kernels, local_step(): pl.pallas_call(write_out, out_shape=[jax.ShapeDtypeStruct(o.shape, o.dtyp...  3.16 us

profile of v6, /device:TPU:1, one launch (start us, length us, event | category | flops | bytes accessed | tf_op | source)
XLA Modules:
  0.0 87.8 jit_solution(10439632816606332024)
XLA Ops:
  0.6 84.0 %verify.1 = (f32[4,1024]{1,0:T(4,128)S(1)}, f32[1,1024]{1,0:T(1,128)S(1)}, f32[8192,128]{1,0:T(8,128)S(1)}, f32[1024,256]{1,0:T(8,128)S(1)}, f32[4,8,128]{2,1,0:T(8,128)S(1)}) custom-call(bf16[5,1024,4096]{2,1,0:T(8,128)(2,1)} %bitcast.16, bf16[4096,256]{1,0:T(8,128)(2,1)} %w_ref.1, f32[8,128,8,128]{3,2,1,0:T(8,128)} %bitcast.17, s32[4,1024]{1,0:T(4,128)} %bitcast.18), custom_call_target="tpu_custom_call" | custom-call | tf_op jit(solution)/shard_map/verify/pallas_call | solution.py:360
  84.7 3.2 %write_out.1 = (f32[4,1024]{1,0:T(4,128)}, f32[1,1024]{1,0:T(1,128)}, f32[128,8,8,128]{3,2,1,0:T(8,128)}, f32[1024,256]{1,0:T(8,128)}) custom-call(f32[4,1024]{1,0:T(4,128)S(1)} %get-tuple-element.13.acc_ref, f32[1,1024]{1,0:T(1,128)S(1)} %get-tuple-element.14.exp_ref, f32[128,8,8,128]{3,2,1,0:T(8,128)S(1)} %bitcast.15, ...), custom_call_target="tpu_custom_call" | custom-call | tf_op jit(solution)/shard_map/write_out/pallas_call | solution.py:394

commit v7 on v6

--- a/solution.py
+++ b/solution.py
@@ -12,15 +12,15 @@
 MESH = pl.DeviceIdType.MESH
 F32 = jnp.float32
 LANES = 128
-CHUNKS = ((0, 3), (3, 1), (4, 1), (5, 2), (7, 1))
+CHUNKS = ((0, 2), (2, 1), (3, 1), (4, 2), (6, 1), (7, 1))
 ROWS = 256
 NBUF = 3
 EARLY = 3
 
 
 def kernel(dims, h_ref, w_ref, q_ref, xin_ref, acc_ref, exp_ref, zr, z4, rz_ref,
-           hbuf, wbuf, x_ref, qsrc, qdst, zb, st_send, st_recv, ag_send, ag_recv, zs_send, zs_recv, h_sem, w_sem, q_sem,
-           x_sem, bulk_ss, bulk_rs, st_ss, st_rs, ag_ss, ag_rs, zs_ss, zs_rs):
+           hbuf, wbuf, x_ref, qsrc, qdst, zb, st_send, st_part, st_recv, ag_send, ag_recv, zs_send, zs_recv, h_sem, w_sem, q_sem,
+           x_sem, bulk_ss, bulk_rs, st_ss, st_rs, ag_ss, ag_rs, pair_ss, pair_rs, zs_ss, zs_rs):
     na, nb = dims
     nd = na * nb
     me_a, me_b = lax.axis_index("tpa"), lax.axis_index("tpb")
@@ -178,49 +178,78 @@
     lax.fori_loop(0, EARLY, matmul, 0)
     pl.semaphore_wait(barrier, nd - 1)
     send_bulk(0)
+
+    @pl.when(me_a == 0)
+    def _():
+        send_bulk(1)
+
     lax.fori_loop(EARLY, npos * per_pos, matmul, 0)
 
     my_unit = (me_b * 43) % nb
-    is_owner = my_unit < nunit
+    is_owner = (my_unit < nunit) & (me_a == 1)
+    partner = {"tpa": cores[1], "tpb": me_b}
+    pair_stats = pltpu.make_async_remote_copy(src_ref=st_send, dst_ref=st_part, send_sem=pair_ss, recv_sem=pair_rs,
+                                              device_id=partner, device_id_type=MESH)
+    pair_answers = pltpu.make_async_remote_copy(src_ref=ag_recv, dst_ref=ag_recv, send_sem=pair_ss, recv_sem=ag_rs,
+                                                device_id=partner, device_id_type=MESH)
+
+    @pl.when(me_a == 0)
+    def _():
+        pair_stats.start()
+        for g in range(2, len(CHUNKS)):
+            send_bulk(g)
+
+    def merge(u, carry):
+        mine, other = st_send[u], st_part[u]
+        top = jnp.maximum(mine[0:1], other[0:1])
+        total = mine[1:2] * jnp.exp(mine[0:1] - top) + other[1:2] * jnp.exp(other[0:1] - top)
+        st_send[u] = jnp.where(sub4 == 0, top, jnp.where(sub4 == 1, total, mine + other))
+        return carry
 
     def send_stats(u, carry):
         chip = (u * 3) % nb
-        for a in range(na):
-            @pl.when((chip != me_b) | (me_a != a))
-            def _():
-                pltpu.make_async_remote_copy(src_ref=st_send.at[u], dst_ref=st_recv.at[me], send_sem=st_ss,
-                                             recv_sem=st_rs, device_id={"tpa": a, "tpb": chip},
-                                             device_id_type=MESH).start()
+
+        @pl.when(chip != me_b)
+        def _():
+            pltpu.make_async_remote_copy(src_ref=st_send.at[u], dst_ref=st_recv.at[me_b], send_sem=st_ss,
+                                         recv_sem=st_rs, device_id={"tpa": me_a, "tpb": chip},
+                                         device_id_type=MESH).start()
         return carry
 
-    lax.fori_loop(0, nunit, send_stats, 0)
-    send_bulk(1)
-
-    @pl.when(is_owner)
-    def _():
-        pltpu.make_async_copy(st_send.at[my_unit], st_recv.at[me], st_rs).start()
-        pltpu.make_async_copy(st_recv, st_recv, st_rs).wait()
-        mx = lax.fori_loop(0, nd, lambda s, m: jnp.maximum(m, st_recv[s]), st_recv[0], unroll=8)[0:1]
-
-        def add(s, carry):
-            t = st_recv[s]
-            es, zp, qq = carry
-            return es + jnp.exp(t[0:1] - mx) * t[1:2], zp + t[2:3], qq + t[3:4]
-
-        zero = jnp.zeros((1, LANES), F32)
-        es, zp, qq = lax.fori_loop(0, nd, add, (zero, zero, zero), unroll=8)
-        accept = jnp.minimum(1.0, jnp.exp(zp - mx) / es / qq)
-        ag_send[...] = jnp.where(sub4 == 0, mx, jnp.where(sub4 == 1, 1.0 / es, accept))
-        pltpu.make_async_copy(ag_send, ag_recv.at[my_unit], ag_rs).start()
-        each_peer(lambda f, ident: pltpu.make_async_remote_copy(
-            src_ref=ag_send, dst_ref=ag_recv.at[my_unit], send_sem=ag_ss, recv_sem=ag_rs, device_id=ident,
-            device_id_type=MESH).start(), far=True, own_core=True)
-
-    send_bulk(2)
+    @pl.when(me_a == 1)
+    def _():
+        pair_stats.wait_recv()
+        lax.fori_loop(0, nunit, merge, 0, unroll=4)
+        lax.fori_loop(0, nunit, send_stats, 0)
+        send_bulk(1)
+
+        @pl.when(is_owner)
+        def _():
+            pltpu.make_async_copy(st_send.at[my_unit], st_recv.at[me_b], st_rs).start()
+            pltpu.make_async_copy(st_recv, st_recv, st_rs).wait()
+            mx = lax.fori_loop(0, nb, lambda s, m: jnp.maximum(m, st_recv[s]), st_recv[0], unroll=8)[0:1]
+
+            def add(s, carry):
+                t = st_recv[s]
+                es, zp, qq = carry
+                return es + jnp.exp(t[0:1] - mx) * t[1:2], zp + t[2:3], qq + t[3:4]
+
+            zero = jnp.zeros((1, LANES), F32)
+            es, zp, qq = lax.fori_loop(0, nb, add, (zero, zero, zero), unroll=8)
+            accept = jnp.minimum(1.0, jnp.exp(zp - mx) / es / qq)
+            ag_send[...] = jnp.where(sub4 == 0, mx, jnp.where(sub4 == 1, 1.0 / es, accept))
+            pltpu.make_async_copy(ag_send, ag_recv.at[my_unit], ag_rs).start()
+            each_peer(lambda f, ident: pltpu.make_async_remote_copy(
+                src_ref=ag_send, dst_ref=ag_recv.at[my_unit], send_sem=ag_ss, recv_sem=ag_rs, device_id=ident,
+                device_id_type=MESH).start(), far=True, own_core=True)
 
     pltpu.make_async_copy(ag_recv, ag_recv, ag_rs).wait()
-    for g in range(3, len(CHUNKS)):
-        send_bulk(g)
+
+    @pl.when(me_a == 1)
+    def _():
+        pair_answers.start()
+        for g in range(2, len(CHUNKS)):
+            send_bulk(g)
 
     def stat_rows(blk, k):
         return jnp.concatenate([ag_recv[blk * npos + i, k:k + 1, :] for i in range(ndraft)], axis=0)
@@ -265,13 +294,13 @@
             part = accs[c][:4] + accs[c][4:]
             zs_send[0, (c0 + c) // 2, ((c0 + c) % 2) * 4:((c0 + c) % 2) * 4 + 4] = part
 
-    half = CHUNKS[2][0]
+    half = CHUNKS[3][0]
     probs(0, half)
-    for g in range(2):
+    for g in range(3):
         wait_bulk(g)
         excess(g)
     probs(half, per_src - half)
-    for g in range(2, len(CHUNKS)):
+    for g in range(3, len(CHUNKS)):
         wait_bulk(g)
         excess(g)
 
@@ -302,15 +331,15 @@
     for g, (c0, n) in enumerate(CHUNKS):
         drain(qsrc.at[pl.ds(c0, n), pl.ds(0, nd - 1)], bulk_ss.at[g])
 
+    drain(st_send, pair_ss)
+
     @pl.when(is_owner)
     def _():
-        drain(st_send, st_ss)
         drain(st_send.at[pl.ds(0, nunit - 1)], st_ss)
         drain(st_recv.at[pl.ds(0, nb - 1)], ag_ss)
 
-    @pl.when(jnp.logical_not(is_owner))
-    def _():
-        drain(st_send, st_ss)
+    @pl.when(jnp.logical_not(is_owner) & (me_a == 1))
+    def _():
         drain(st_send, st_ss)
 
     for t, group in enumerate(axes):
@@ -376,13 +405,14 @@
                 vm((nd, per_src, 8, LANES), F32),
                 vm((ROWS, vloc), F32),
                 vm((nunit, 4, LANES), F32),
-                vm((nd, 4, LANES), F32),
+                vm((nunit, 4, LANES), F32),
+                vm((nb, 4, LANES), F32),
                 vm((4, LANES), F32),
                 vm((nunit, 4, LANES), F32),
                 vm((3, per_src // 2, 8, LANES), F32),
                 vm((13, per_src // 2, 8, LANES), F32),
-                dma((NBUF,)), dma, dma, dma, dma((len(CHUNKS),)), dma((len(CHUNKS),)), dma, dma, dma, dma, dma((3,)),
-                dma((3,)),
+                dma((NBUF,)), dma, dma, dma, dma((len(CHUNKS),)), dma((len(CHUNKS),)), dma, dma, dma, dma, dma, dma,
+                dma((3,)), dma((3,)),
             ],
             compiler_params=pltpu.CompilerParams(collective_id=0, has_side_effects=True,
                                                  vmem_limit_bytes=46 * 1024 * 1024),

time: 88.4 us -> 96.9 us (1.096)
  the two profiles are of different devices: /device:TPU:1 before, /device:TPU:10 now
where the time goes in v7:
time: 96.9 us; the launch traced here: 96.8 us
  Pallas kernels  96.2 us (99%)
    pallas_call x1, Pallas kernels, local_step(): pl.pallas_call(functools.partial(kernel, (na, nb)), out_shape=[jax.ShapeD...  93 us
    pallas_call x1, Pallas kernels, local_step(): pl.pallas_call(write_out, out_shape=[jax.ShapeDtypeStruct(o.shape, o.dtyp...  3.16 us

profile of v7, /device:TPU:10, one launch (start us, length us, event | category | flops | bytes accessed | tf_op | source)
XLA Modules:
  0.0 96.8 jit_solution(18148302712548908841)
XLA Ops:
  0.6 93.0 %verify.1 = (f32[4,1024]{1,0:T(4,128)S(1)}, f32[1,1024]{1,0:T(1,128)S(1)}, f32[8192,128]{1,0:T(8,128)S(1)}, f32[1024,256]{1,0:T(8,128)S(1)}, f32[4,8,128]{2,1,0:T(8,128)S(1)}) custom-call(bf16[5,1024,4096]{2,1,0:T(8,128)(2,1)} %bitcast.16, bf16[4096,256]{1,0:T(8,128)(2,1)} %w_ref.1, f32[8,128,8,128]{3,2,1,0:T(8,128)} %bitcast.17, s32[4,1024]{1,0:T(4,128)} %bitcast.18), custom_call_target="tpu_custom_call" | custom-call | tf_op jit(solution)/shard_map/verify/pallas_call | solution.py:389
  93.7 3.2 %write_out.1 = (f32[4,1024]{1,0:T(4,128)}, f32[1,1024]{1,0:T(1,128)}, f32[128,8,8,128]{3,2,1,0:T(8,128)}, f32[1024,256]{1,0:T(8,128)}) custom-call(f32[4,1024]{1,0:T(4,128)S(1)} %get-tuple-element.13.acc_ref, f32[1,1024]{1,0:T(1,128)S(1)} %get-tuple-element.14.exp_ref, f32[128,8,8,128]{3,2,1,0:T(8,128)S(1)} %bitcast.15, ...), custom_call_target="tpu_custom_call" | custom-call | tf_op jit(solution)/shard_map/write_out/pallas_call | solution.py:424

commit v8 on v6

--- a/solution.py
+++ b/solution.py
@@ -12,9 +12,9 @@
 MESH = pl.DeviceIdType.MESH
 F32 = jnp.float32
 LANES = 128
-CHUNKS = ((0, 3), (3, 1), (4, 1), (5, 2), (7, 1))
+CHUNKS = ((0, 4), (4, 1), (5, 1), (6, 1), (7, 1))
 ROWS = 256
-NBUF = 3
+NBUF = 6
 EARLY = 3
 
 

time: 88.4 us -> 94.8 us (1.072)
  Pallas kernels: 87.2 us -> 93.5 us
    pallas_call x1, Pallas kernels: 84 us -> 90.4 us  [local_step(): pl.pallas_call(functools.partial(kernel, (na, nb)), out_shape=[jax.ShapeD...]
where the time goes in v8:
time: 94.8 us; the launch traced here: 94.2 us
  Pallas kernels  93.5 us (99%)
    pallas_call x1, Pallas kernels, local_step(): pl.pallas_call(functools.partial(kernel, (na, nb)), out_shape=[jax.ShapeD...  90.4 us
    pallas_call x1, Pallas kernels, local_step(): pl.pallas_call(write_out, out_shape=[jax.ShapeDtypeStruct(o.shape, o.dtyp...  3.16 us

profile of v8, /device:TPU:1, one launch (start us, length us, event | category | flops | bytes accessed | tf_op | source)
XLA Modules:
  0.0 94.2 jit_solution(7204793118469565280)
XLA Ops:
  0.6 90.4 %verify.1 = (f32[4,1024]{1,0:T(4,128)S(1)}, f32[1,1024]{1,0:T(1,128)S(1)}, f32[8192,128]{1,0:T(8,128)S(1)}, f32[1024,256]{1,0:T(8,128)S(1)}, f32[4,8,128]{2,1,0:T(8,128)S(1)}) custom-call(bf16[5,1024,4096]{2,1,0:T(8,128)(2,1)} %bitcast.16, bf16[4096,256]{1,0:T(8,128)(2,1)} %w_ref.1, f32[8,128,8,128]{3,2,1,0:T(8,128)} %bitcast.17, s32[4,1024]{1,0:T(4,128)} %bitcast.18), custom_call_target="tpu_custom_call" | custom-call | tf_op jit(solution)/shard_map/verify/pallas_call | solution.py:360
  91.0 3.2 %write_out.1 = (f32[4,1024]{1,0:T(4,128)}, f32[1,1024]{1,0:T(1,128)}, f32[128,8,8,128]{3,2,1,0:T(8,128)}, f32[1024,256]{1,0:T(8,128)}) custom-call(f32[4,1024]{1,0:T(4,128)S(1)} %get-tuple-element.13.acc_ref, f32[1,1024]{1,0:T(1,128)S(1)} %get-tuple-element.14.exp_ref, f32[128,8,8,128]{3,2,1,0:T(8,128)S(1)} %bitcast.15, ...), custom_call_target="tpu_custom_call" | custom-call | tf_op jit(solution)/shard_map/write_out/pallas_call | solution.py:394

commit v9 on v6

--- a/solution.py
+++ b/solution.py
@@ -12,7 +12,7 @@
 MESH = pl.DeviceIdType.MESH
 F32 = jnp.float32
 LANES = 128
-CHUNKS = ((0, 3), (3, 1), (4, 1), (5, 2), (7, 1))
+CHUNKS = ((0, 2), (2, 1), (3, 2), (5, 2), (7, 1))
 ROWS = 256
 NBUF = 3
 EARLY = 3

time: 88.4 us -> 94.7 us (1.071); the launches traced: 87.8 us -> 93 us
  Pallas kernels: 87.2 us -> 92.4 us
    pallas_call x1, Pallas kernels: 84 us -> 89.2 us  [local_step(): pl.pallas_call(functools.partial(kernel, (na, nb)), out_shape=[jax.ShapeD...]
where the time goes in v9:
time: 94.7 us; the launch traced here: 93 us
  Pallas kernels  92.4 us (98%)
    pallas_call x1, Pallas kernels, local_step(): pl.pallas_call(functools.partial(kernel, (na, nb)), out_shape=[jax.ShapeD...  89.2 us
    pallas_call x1, Pallas kernels, local_step(): pl.pallas_call(write_out, out_shape=[jax.ShapeDtypeStruct(o.shape, o.dtyp...  3.16 us

profile of v9, /device:TPU:1, one launch (start us, length us, event | category | flops | bytes accessed | tf_op | source)
XLA Modules:
  0.0 93.0 jit_solution(15352095537795349671)
XLA Ops:
  0.6 89.2 %verify.1 = (f32[4,1024]{1,0:T(4,128)S(1)}, f32[1,1024]{1,0:T(1,128)S(1)}, f32[8192,128]{1,0:T(8,128)S(1)}, f32[1024,256]{1,0:T(8,128)S(1)}, f32[4,8,128]{2,1,0:T(8,128)S(1)}) custom-call(bf16[5,1024,4096]{2,1,0:T(8,128)(2,1)} %bitcast.16, bf16[4096,256]{1,0:T(8,128)(2,1)} %w_ref.1, f32[8,128,8,128]{3,2,1,0:T(8,128)} %bitcast.17, s32[4,1024]{1,0:T(4,128)} %bitcast.18), custom_call_target="tpu_custom_call" | custom-call | tf_op jit(solution)/shard_map/verify/pallas_call | solution.py:360
  89.8 3.2 %write_out.1 = (f32[4,1024]{1,0:T(4,128)}, f32[1,1024]{1,0:T(1,128)}, f32[128,8,8,128]{3,2,1,0:T(8,128)}, f32[1024,256]{1,0:T(8,128)}) custom-call(f32[4,1024]{1,0:T(4,128)S(1)} %get-tuple-element.13.acc_ref, f32[1,1024]{1,0:T(1,128)S(1)} %get-tuple-element.14.exp_ref, f32[128,8,8,128]{3,2,1,0:T(8,128)S(1)} %bitcast.15, ...), custom_call_target="tpu_custom_call" | custom-call | tf_op jit(solution)/shard_map/write_out/pallas_call | solution.py:394
